TPU v7x, 32 devices: a whole 2x2x4 slice. The times are simulated.
32 devices in a mesh: grp: 1, mid: 16 (over z, y, core), off: 2 (over x), sub: 1.
Axes of the slice: x: 2, y: 2, z: 4, core: 2. Of those that a mesh axis runs over, the one named last changes fastest.
Arguments:
- traces: bfloat16 [2, 1024, 1024], P('off', ('grp', 'mid'), 'sub'), may hold values from -6 to 6
- centre_offset: int32 [256], P(('grp', 'mid')), may hold values from 0 to 63
- foot_start: int32 [256, 16], P('grp'), may hold values from 0 to 240
- beam_count: int32 [16], P('grp'), may hold values from 2 to 16, as said below
- operator: bfloat16 [1024, 65536], P('sub', 'mid'), may hold values from -0.1875 to 0.1875
Outputs:
- image: float32 [256, 256], P(('grp', 'mid'))
Inputs may be any that keep to these rules, and one draw needn't show every extreme that they name: `beam_count`: the live beams of all tiles sum to exactly 128, and the largest count is exactly 16.
All inputs are finite; a program needn't handle non-finite values.
Results may differ from a plain program's by a relative error of at most 0.0028.
Values may be sent and summed in bfloat16 or wider, within the bound.
No kernel may reach another device: no remote copies, remote signals or barrier semaphores. Data moves between devices by JAX's collectives and lax.ppermute only.
A program may use at most 64 MiB of HBM per device.

v0:
```python
import math

import jax
import jax.numpy as jnp
from jax import lax
from jax.sharding import PartitionSpec as P

NT = 1024
P_SIZE = 16
FL = 16
DEPTH = 256
HALF = 16
CB_DEV = 16


def padded_2(cells, sides, width):
    for axis, dim in sides:
        count = lax.axis_size(axis)
        ends = count - 1
        head = lax.slice_in_dim(cells, 0, width, axis=dim)
        tail = lax.slice_in_dim(cells, cells.shape[dim] - width, cells.shape[dim], axis=dim)
        cells = jnp.concatenate(
            [
                lax.ppermute(tail, axis, [(i, (i + 1) % count) for i in range(ends)]),
                cells,
                lax.ppermute(head, axis, [((i + 1) % count, i) for i in range(ends)]),
            ],
            axis=dim,
        )
    return cells


def dft_rows(first_row, row_count, freq_block):
    sample_index = first_row + jnp.arange(row_count, dtype=jnp.int32)[:, None]
    column = jnp.arange(NT, dtype=jnp.int32)[None, :]
    within = column % (2 * freq_block)
    frequency = column // (2 * freq_block) * freq_block + within % freq_block
    phase_angle = 2.0 * math.pi / NT * (sample_index * frequency % NT).astype(jnp.float32)
    values = jnp.where(within // freq_block == 1, -jnp.sin(phase_angle), jnp.cos(phase_angle))
    return values / math.sqrt(NT)


def slant_weights(frequency):
    offsets = jnp.arange(-HALF, HALF + 1, dtype=jnp.int32).astype(jnp.float32)
    taper = jnp.exp(-0.5 * (1.5 * offsets / HALF) ** 2)
    taper = taper / jnp.sqrt(jnp.sum(taper * taper))
    slopes = 0.25 * (jnp.arange(P_SIZE, dtype=jnp.int32).astype(jnp.float32) - 0.5 * (P_SIZE - 1))
    theta = (
        2.0
        * math.pi
        / NT
        * slopes[:, None, None]
        * offsets[None, :, None]
        * frequency.astype(jnp.float32)[None, None, :]
    )
    return (taper[None, :, None] * jnp.cos(theta), taper[None, :, None] * jnp.sin(theta))


def form_beams(windows_real, windows_imag, cos_weight, sin_weight):
    high = lax.Precision.HIGHEST
    beam_real = jnp.einsum("pxf,bxf->bpf", cos_weight, windows_real, precision=high) + jnp.einsum(
        "pxf,bxf->bpf", sin_weight, windows_imag, precision=high
    )
    beam_imag = jnp.einsum("pxf,bxf->bpf", cos_weight, windows_imag, precision=high) - jnp.einsum(
        "pxf,bxf->bpf", sin_weight, windows_real, precision=high
    )
    return (beam_real, beam_imag)


def live_rows(beam_count, per_tile, live_total):
    tile_ends = jnp.cumsum(beam_count)
    position = jnp.arange(live_total, dtype=jnp.int32)
    owner = jnp.sum((position[:, None] >= tile_ends[None, :]).astype(jnp.int32), axis=1)
    first = tile_ends - beam_count
    match = owner[:, None] == jnp.arange(beam_count.shape[0], dtype=jnp.int32)[None, :]
    chosen = jnp.sum(jnp.where(match, first[None, :], 0), axis=1)
    return owner * per_tile + position - chosen


def spread_slopes(beams, mid_count):
    return jnp.repeat(beams, mid_count // P_SIZE, axis=1)[:, :, None, :]


def shards(traces, centre_offset, foot_start, beam_count, operator):
    high = lax.Precision.HIGHEST
    mid_count = lax.axis_size("mid")
    mid_index = lax.axis_index("mid")
    sub_index = lax.axis_index("sub")
    samples = traces.shape[2]
    freq_block = samples // 2
    dft_table = dft_rows(sub_index * samples, samples, freq_block)
    partial_value = jnp.dot(traces[0].astype(jnp.float32), dft_table, precision=high)
    spectrum = lax.psum_scatter(partial_value, "sub", scatter_dimension=1, tiled=True)
    padded = padded_2(spectrum, (("mid", 0),), HALF)
    window_index = centre_offset[:, None] + jnp.arange(2 * HALF + 1, dtype=jnp.int32)[None, :]
    windows = padded[window_index]
    frequency = sub_index * freq_block + jnp.arange(freq_block, dtype=jnp.int32)
    cos_weight, sin_weight = slant_weights(frequency)
    beam_real, beam_imag = form_beams(
        windows[:, :, :freq_block], windows[:, :, freq_block:], cos_weight, sin_weight
    )
    live_here = lax.dynamic_index_in_dim(beam_count, mid_index, 0, keepdims=False)
    alive = jnp.arange(CB_DEV, dtype=jnp.int32) < live_here
    beams = jnp.where(
        alive[:, None, None], jnp.concatenate([beam_real, beam_imag], axis=2), 0.0
    ).astype(jnp.bfloat16)
    columns = operator.shape[1]
    slope_count = max(1, P_SIZE // mid_count)
    footprint_size = FL * DEPTH
    first_column = mid_index * columns
    slope_first = first_column // footprint_size
    lateral_first = first_column % footprint_size // DEPTH
    lateral_count = columns // (slope_count * DEPTH)
    starts = lax.dynamic_slice_in_dim(foot_start, slope_first, slope_count, 1)
    kernels = operator.reshape(samples, slope_count, lateral_count * DEPTH)
    outgoing = spread_slopes(beams, mid_count)
    received = lax.all_to_all(outgoing, "mid", split_axis=1, concat_axis=0, tiled=True)
    row_total = received.shape[0]
    received = received.reshape(row_total, slope_count, samples)
    chosen = live_rows(beam_count, CB_DEV, row_total // 2)
    received = received[chosen]
    starts = starts[chosen]
    centres_all = CB_DEV * mid_count
    block_rows = received.shape[0] // 8
    lateral_steps = lateral_first + jnp.arange(lateral_count, dtype=jnp.int32)
    weight_scale = 1.0 / math.sqrt(FL * P_SIZE)

    def add_block(block, partial_image):
        block_beams = lax.dynamic_slice_in_dim(received, block * block_rows, block_rows, 0)
        block_starts = lax.dynamic_slice_in_dim(starts, block * block_rows, block_rows, 0)
        footprint = (
            jnp.einsum(
                "rsk,ksc->rsc",
                block_beams,
                kernels,
                preferred_element_type=jnp.float32,
                precision=None,
            )
            * weight_scale
        )
        target = (block_starts[:, :, None] + lateral_steps[None, None, :]).reshape(-1)
        return partial_image.at[target].add(footprint.reshape(-1, DEPTH))

    partial_image = lax.fori_loop(0, 8, add_block, jnp.zeros((centres_all, DEPTH), jnp.float32))
    tile_part = lax.psum_scatter(partial_image, "mid", scatter_dimension=0, tiled=True)
    image_tile = lax.psum(tile_part, ("off", "sub"))
    return image_tile


def solution(mesh):
    return jax.shard_map(
        shards,
        mesh=mesh,
        in_specs=(
            P("off", ("grp", "mid"), "sub"),
            P(("grp", "mid")),
            P("grp", None),
            P("grp"),
            P("sub", "mid"),
        ),
        out_specs=P(("grp", "mid"), None),
        check_vma=False,
    )
```

profile of v0, /device:TPU:0, one launch (start us, length us, event | category | flops | bytes accessed | tf_op | source)
XLA Modules:
  0.0 302.9 jit_solution(10258780660640773657)
XLA Ops:
  6.6 0.9 copy-done
  7.4 19.2 %fusion.60 = f32[64,1024]{1,0:T(8,128)S(1)} fusion(s32[1024]{0:T(1024)S(1)} %fusion.67, pred[1024]{0:T(1024)(128)(4,1)S(1)} %fusion.64, bf16[1,64,1024]{2,1,0:T(8,128)(2,1)S(1)} %copy-done), kind=kOutput, calls=%fused_computation.61 | convolution fusion | flops 823132160 | bytes 398336 | tf_op jit(solution)/shard_map/dot_general | solution.py:92
  26.7 2.4 collective-permute-start
  29.1 1.5 collective-permute-start.1
  30.6 0.6 multiply_reduce_fusion
  32.2 0.6 dynamic_slice.24
  32.8 0.6 iota_compare_fusion.2
  33.4 0.9 collective-permute-done.1
  34.4 2.5 gather_fusion.1
  36.8 1.7 reshape.394
  38.5 2.0 fusion.81
  40.5 3.7 %copy.23 = f32[16,33,512]{1,0,2:T(8,128)} copy(f32[16,33,512]{2,1,0:T(8,128)S(1)} %get-tuple-element.148) | data formatting | bytes 2162688
  44.2 3.8 %copy.24 = f32[16,33,512]{1,0,2:T(8,128)} copy(f32[16,33,512]{2,1,0:T(8,128)S(1)} %get-tuple-element.149) | data formatting | bytes 2162688
  48.0 24.9 %fusion.16 = f32[512,16,16]{2,1,0:T(8,128)S(1)} fusion(f32[16,33,512]{1,0,2:T(8,128)} %copy.23, f32[512]{0:T(512)S(1)} %iota_convert_fusion, f32[16,33]{1,0:T(8,128)S(1)} %broadcast_multiply_fusion, f32[33]{0:T(128)S(1)} %broadcast_divide_fusion), kind=kOutput, calls=%fused_computation.24 | convolution fusion | flops 52445184 | bytes 1609924 | tf_op jit(solution)/shard_map/pxf,bxf->bpf/dot_general | solution.py:61
  72.9 22.2 %fusion.14 = f32[512,16,16]{2,1,0:T(8,128)S(1)} fusion(f32[16,33,512]{1,0,2:T(8,128)S(1)} %copy-done.3, f32[512]{0:T(512)S(1)} %iota_convert_fusion, f32[16,33]{1,0:T(8,128)S(1)} %broadcast_multiply_fusion, f32[33]{0:T(128)S(1)} %broadcast_divide_fusion), kind=kOutput, calls=%fused_computation.23 | convolution fusion | flops 52445184 | bytes 1609924 | tf_op jit(solution)/shard_map/pxf,bxf->bpf/dot_general | solution.py:64
  95.1 23.7 %add_bitcast_fusion = bf16[16,16,1,512]{1,0,3,2:T(8,128)(2,1)S(1)} fusion(f32[512,16,16]{2,1,0:T(8,128)S(1)} %fusion.16, f32[16,33,512]{1,0,2:T(8,128)S(1)} %copy-done.3, f32[512]{0:T(512)S(1)} %iota_convert_fusion, f32[16,33]{1,0:T(8,128)S(1)} %broadcast_multiply_fusion, f32[33]{0:T(128)S(1)} %broadcast_divide_fusion), kind=kOutput, calls=%fused_computation.32 | convolution fusion | flops 52707328 | bytes 1872068 | tf_op jit(solution)/shard_map/pxf,bxf->bpf/dot_general | solution.py:61
  118.9 23.7 %subtract_bitcast_fusion = bf16[16,16,1,512]{1,0,3,2:T(8,128)(2,1)S(1)} fusion(f32[512,16,16]{2,1,0:T(8,128)S(1)} %fusion.14, f32[16,33,512]{1,0,2:T(8,128)S(1)} %copy-done.2, f32[512]{0:T(512)S(1)} %iota_convert_fusion, f32[16,33]{1,0:T(8,128)S(1)} %broadcast_multiply_fusion, f32[33]{0:T(128)S(1)} %broadcast_divide_fusion), kind=kOutput, calls=%fused_computation.31 | convolution fusion | flops 52707328 | bytes 1872068 | tf_op jit(solution)/shard_map/pxf,bxf->bpf/dot_general | solution.py:64
  142.6 2.6 maximum_select_fusion
  145.2 5.7 %copy.22 = bf16[16,16,1,1024]{3,0,2,1:T(8,128)(2,1)} copy(bf16[16,16,1,1024]{1,0,3,2:T(8,128)(2,1)} %maximum_select_fusion) | data formatting | bytes 1048576 | tf_op jit(solution)/shard_map/jit(_where)/select_n | solution.py:104
  150.8 8.4 %all-to-all-start = ((bf16[16,16,1,1024]{3,0,2,1:T(8,128)(2,1)}), bf16[16,16,1,1024]{3,0,2,1:T(8,128)(2,1)S(1)}, u32[]{:S(2)}, u32[]{:S(2)}) async-start(bf16[16,16,1,1024]{3,0,2,1:T(8,128)(2,1)} %copy.22), calls=%async_computation | async-start | bytes 1048576 | tf_op jit(solution)/shard_map/all_to_all | solution.py:117
  159.2 0.3 reduce-scatter.2.cloned.1.call-start
  159.7 0.1 reduce.1
  159.8 0.7 constant_dynamic-slice_fusion
  160.7 1.3 gather_fusion
  162.0 11.5 %all-to-all-done = bf16[16,16,1,1024]{3,0,2,1:T(8,128)(2,1)S(1)} async-done(((bf16[16,16,1,1024]{3,0,2,1:T(8,128)(2,1)}), bf16[16,16,1,1024]{3,0,2,1:T(8,128)(2,1)S(1)}, u32[]{:S(2)}, u32[]{:S(2)}) %all-to-all-start) | async-done | bytes 524320 | tf_op jit(solution)/shard_map/all_to_all | solution.py:117
  173.5 0.9 gather_fusion.2
  174.4 56.2 %while.14 = (s32[]{:T(128)}, f32[256,256]{1,0:T(8,128)S(1)}, s32[128,1]{0,1:T(1,128)S(1)}, bf16[128,1,1024]{2,0,1:T(8,128)(2,1)S(1)}, bf16[1024,1,4096]{2,0,1:T(...) while((s32[]{:T(128)}, f32[256,256]{1,0:T(8,128)S(1)}, ...), condition=%wide.region_6.7_spmd.clone, body=%wide.region_4.6_spmd.clone.sunk | while | flops 134349840 | bytes 10000863 | solution.py:144
  174.4 4.6 %fusion.92 = f32[16,1,4096]{2,0,1:T(8,128)S(1)} fusion(bf16[1024,1,4096]{2,0,1:T(8,128)(2,1)} %get-tuple-element.213, bf16[128,1,1024]{2,0,1:T(8,128)(2,1)S(1)} %get-tuple-element.212, s32[]{:T(128)S(6)} %select_n.211), kind=kOutput, calls=%fused_computation.8.clone.1 | convolution fusion | flops 134283264 | bytes 8683524 | tf_op jit(solution)/shard_map/while/body/eval_jaxpr/rsk,ksc->rsc/dot_general | solution.py:132
  179.1 0.1 add_reduce_fusion.2
  179.3 2.1 scatter_fusion
  181.4 4.6 %fusion.92 = f32[16,1,4096]{2,0,1:T(8,128)S(1)} fusion(bf16[1024,1,4096]{2,0,1:T(8,128)(2,1)} %get-tuple-element.213, bf16[128,1,1024]{2,0,1:T(8,128)(2,1)S(1)} %get-tuple-element.212, s32[]{:T(128)S(6)} %select_n.211), kind=kOutput, calls=%fused_computation.8.clone.1 | convolution fusion | flops 134283264 | bytes 8683524 | tf_op jit(solution)/shard_map/while/body/eval_jaxpr/rsk,ksc->rsc/dot_general | solution.py:132
  186.1 0.1 add_reduce_fusion.2
  186.3 2.1 scatter_fusion
  188.4 4.6 %fusion.92 = f32[16,1,4096]{2,0,1:T(8,128)S(1)} fusion(bf16[1024,1,4096]{2,0,1:T(8,128)(2,1)} %get-tuple-element.213, bf16[128,1,1024]{2,0,1:T(8,128)(2,1)S(1)} %get-tuple-element.212, s32[]{:T(128)S(6)} %select_n.211), kind=kOutput, calls=%fused_computation.8.clone.1 | convolution fusion | flops 134283264 | bytes 8683524 | tf_op jit(solution)/shard_map/while/body/eval_jaxpr/rsk,ksc->rsc/dot_general | solution.py:132
  193.3 2.1 scatter_fusion
  195.5 4.6 %fusion.92 = f32[16,1,4096]{2,0,1:T(8,128)S(1)} fusion(bf16[1024,1,4096]{2,0,1:T(8,128)(2,1)} %get-tuple-element.213, bf16[128,1,1024]{2,0,1:T(8,128)(2,1)S(1)} %get-tuple-element.212, s32[]{:T(128)S(6)} %select_n.211), kind=kOutput, calls=%fused_computation.8.clone.1 | convolution fusion | flops 134283264 | bytes 8683524 | tf_op jit(solution)/shard_map/while/body/eval_jaxpr/rsk,ksc->rsc/dot_general | solution.py:132
  200.4 2.1 scatter_fusion
  202.5 4.6 %fusion.92 = f32[16,1,4096]{2,0,1:T(8,128)S(1)} fusion(bf16[1024,1,4096]{2,0,1:T(8,128)(2,1)} %get-tuple-element.213, bf16[128,1,1024]{2,0,1:T(8,128)(2,1)S(1)} %get-tuple-element.212, s32[]{:T(128)S(6)} %select_n.211), kind=kOutput, calls=%fused_computation.8.clone.1 | convolution fusion | flops 134283264 | bytes 8683524 | tf_op jit(solution)/shard_map/while/body/eval_jaxpr/rsk,ksc->rsc/dot_general | solution.py:132
  207.4 2.1 scatter_fusion
  209.5 4.6 %fusion.92 = f32[16,1,4096]{2,0,1:T(8,128)S(1)} fusion(bf16[1024,1,4096]{2,0,1:T(8,128)(2,1)} %get-tuple-element.213, bf16[128,1,1024]{2,0,1:T(8,128)(2,1)S(1)} %get-tuple-element.212, s32[]{:T(128)S(6)} %select_n.211), kind=kOutput, calls=%fused_computation.8.clone.1 | convolution fusion | flops 134283264 | bytes 8683524 | tf_op jit(solution)/shard_map/while/body/eval_jaxpr/rsk,ksc->rsc/dot_general | solution.py:132
  214.4 2.1 scatter_fusion
  216.5 4.6 %fusion.92 = f32[16,1,4096]{2,0,1:T(8,128)S(1)} fusion(bf16[1024,1,4096]{2,0,1:T(8,128)(2,1)} %get-tuple-element.213, bf16[128,1,1024]{2,0,1:T(8,128)(2,1)S(1)} %get-tuple-element.212, s32[]{:T(128)S(6)} %select_n.211), kind=kOutput, calls=%fused_computation.8.clone.1 | convolution fusion | flops 134283264 | bytes 8683524 | tf_op jit(solution)/shard_map/while/body/eval_jaxpr/rsk,ksc->rsc/dot_general | solution.py:132
  221.4 2.1 scatter_fusion
  223.5 4.6 %fusion.92 = f32[16,1,4096]{2,0,1:T(8,128)S(1)} fusion(bf16[1024,1,4096]{2,0,1:T(8,128)(2,1)} %get-tuple-element.213, bf16[128,1,1024]{2,0,1:T(8,128)(2,1)S(1)} %get-tuple-element.212, s32[]{:T(128)S(6)} %select_n.211), kind=kOutput, calls=%fused_computation.8.clone.1 | convolution fusion | flops 134283264 | bytes 8683524 | tf_op jit(solution)/shard_map/while/body/eval_jaxpr/rsk,ksc->rsc/dot_general | solution.py:132
  228.4 2.1 scatter_fusion
  230.5 0.7 copy-done.1
  231.3 55.4 %reduce-scatter.2.cloned.1.call-done = f32[16,256]{1,0:T(8,128)} async-done(((f32[256,256]{1,0:T(8,128)}), f32[16,256]{1,0:T(8,128)}) %reduce-scatter.2.cloned.1.call-update) | async-done | bytes 16400 | tf_op jit(solution)/shard_map/reduce_scatter | solution.py:145
  286.7 9.4 %psum.7 = f32[16,256]{1,0:T(8,128)} all-reduce(f32[16,256]{1,0:T(8,128)} %reduce-scatter.2.cloned.1.call-done), channel_id=1, replica_groups=mesh['grp'=1,'mid'=16,'off'=2,'sub'=1] {'off','sub'}, use_global_device_ids=true, to_apply=%region_8.9 | all-reduce | flops 4096 | bytes 32768 | tf_op jit(solution)/shard_map/psum | solution.py:146
  (78 shorter events, 3.0 us)
Async XLA Ops:
  6.5 0.9 copy-start
  7.4 23.8 %copy-start.4 = (s32[16]{0:T(128)S(1)}, s32[16]{0:T(128)}, u32[]{:S(2)}) copy-start(s32[16]{0:T(128)} %param.8) | copy-start | bytes 196
  7.4 24.7 %copy-start.5 = (s32[16]{0:T(128)S(1)}, s32[16]{0:T(128)}, u32[]{:S(2)}) copy-start(s32[16]{0:T(128)} %param.10) | copy-start | bytes 196
  26.7 6.7 %collective-permute-start = (f32[16,1024]{1,0:T(8,128)S(1)}, f32[16,1024]{1,0:T(8,128)S(1)}, u32[]{:S(2)}, u32[]{:S(2)}) collective-permute-start(f32[16,1024]{1,0:T(8,128)S(1)} %get-tuple-element.150), channel_id=1, source_target_pairs={{0,2},{2,4},{4,6},{6,8},{8,10},{10,12},{12,14},{14,16},{16,18},{18... | collective-permute-start | bytes 196616 | tf_op jit(solution)/shard_map/ppermute | solution.py:24
  29.1 5.3 %collective-permute-start.1 = (f32[16,1024]{1,0:T(8,128)S(1)}, f32[16,1024]{1,0:T(8,128)S(1)}, u32[]{:S(2)}, u32[]{:S(2)}) collective-permute-start(f32[16,1024]{1,0:T(8,128)S(1)} %get-tuple-element.151), channel_id=1, source_target_pairs={{2,0},{4,2},{6,4},{8,6},{10,8},{12,10},{14,12},{16,14},{18,16},{20... | collective-permute-start | bytes 196616 | tf_op jit(solution)/shard_map/ppermute | solution.py:26
  48.0 24.9 %copy-start.3 = (f32[16,33,512]{1,0,2:T(8,128)S(1)}, f32[16,33,512]{1,0,2:T(8,128)}, u32[]{:S(2)}) copy-start(f32[16,33,512]{1,0,2:T(8,128)} %copy.24) | copy-start | bytes 3244036
  95.1 23.8 %copy-start.2 = (f32[16,33,512]{1,0,2:T(8,128)S(1)}, f32[16,33,512]{1,0,2:T(8,128)}, u32[]{:S(2)}) copy-start(f32[16,33,512]{1,0,2:T(8,128)} %copy.23) | copy-start | bytes 3244036
  150.8 22.7 %all-to-all-start = ((bf16[16,16,1,1024]{3,0,2,1:T(8,128)(2,1)}), bf16[16,16,1,1024]{3,0,2,1:T(8,128)(2,1)S(1)}, u32[]{:S(2)}, u32[]{:S(2)}) async-start(bf16[16,16,1,1024]{3,0,2,1:T(8,128)(2,1)} %copy.22), calls=%async_computation | async-start | bytes 1048576 | tf_op jit(solution)/shard_map/all_to_all | solution.py:117
  159.2 127.5 %reduce-scatter.2.cloned.1.call-start = ((), (), s32[]{:S(2)}) async-start(), calls=%async_computation.2 | async-start | bytes 278528 | tf_op jit(solution)/shard_map/reduce_scatter | solution.py:145
  230.5 0.7 copy-start.1
Sparse Core Ops, SparseCore 0:
  231.4 55.2 reduce-scatter.1
where the time goes:
time: 304 us; the launch traced here: 303 us
  matrix products  150 us (49%)
  waiting for transfers between devices  67.9 us (22%)
  local copies, waits for them, and re-layouts  26.1 us (9%)
  other arithmetic  21.8 us (7%)
  between operations  14.4 us (5%)
  starting transfers between devices  12.5 us (4%)
  blocking collectives  9.37 us (3%)
    reduce_scatter x1, waiting for transfers between devices, shards(): lax.psum_scatter(partial_image, 'mid', scatter_dimension=0, tiled=True)  55.4 us
    dot_general x8, matrix products, add_block(): jnp.einsum('rsk,ksc->rsc', block_beams, kernels, preferred_element_type=j...  36.7 us
    dot_general x1, matrix products, form_beams(): jnp.einsum('pxf,bxf->bpf', cos_weight, windows_real, precision=high)  24.9 us
    dot_general x1, matrix products, form_beams(): jnp.einsum('pxf,bxf->bpf', sin_weight, windows_imag, precision=high)  23.7 us
    dot_general x1, matrix products, form_beams(): jnp.einsum('pxf,bxf->bpf', sin_weight, windows_real, precision=high)  23.7 us
    dot_general x1, matrix products, form_beams(): jnp.einsum('pxf,bxf->bpf', cos_weight, windows_imag, precision=high)  22.2 us
    dot_general x1, matrix products, shards(): jnp.dot(traces[0].astype(jnp.float32), dft_table, precision=high)  19.2 us
    scatter-add x8, other arithmetic, add_block(): return partial_image.at[target].add(footprint.reshape(-1, DEPTH))  16.6 us
  transfers between devices with their start and end apart: 4, of which 3 were waited for; matrix products, arithmetic and copies ran while one was open for 1% of the time, Pallas kernels for 0%

commit v1 on v0

v1 whole, which is shorter than its diff:
```python
import functools
import math

import jax
import jax.numpy as jnp
import numpy as np
from jax import lax
from jax.experimental import pallas as pl
from jax.experimental.pallas import tpu as pltpu
from jax.sharding import PartitionSpec as P

NT = 1024
P_SIZE = 16
FL = 16
DEPTH = 256
HALF = 16
CB_DEV = 16
PAIRS = P_SIZE // 2
LANES = 128
GROUPS = 4
BF16 = jnp.bfloat16
F32 = jnp.float32


def split_bf16(values):
    high = values.astype(BF16)
    return high, (values - high.astype(values.dtype)).astype(BF16)


def quarter_table():
    phase = np.arange(NT // 4)[:, None] * np.arange(NT // 2)[None, :] % NT
    angle = 2.0 * np.pi / NT * phase
    table = np.concatenate([np.cos(angle), -np.sin(angle)], axis=1) / np.sqrt(NT)
    high = table.astype(BF16)
    return high, (table - high.astype(np.float64)).astype(BF16)


def offset_taper(offsets):
    window = np.exp(-0.5 * (1.5 * np.arange(-HALF, HALF + 1) / HALF) ** 2)
    return np.exp(-0.5 * (1.5 * offsets / HALF) ** 2) / np.sqrt(np.sum(window**2))


def slant_tables():
    offsets = np.arange(HALF + 1)
    slopes = 0.25 * (np.arange(PAIRS) - 0.5 * (P_SIZE - 1))
    theta = (
        2.0 * np.pi / NT * slopes[None, :, None] * offsets[:, None, None] * np.arange(NT // 2)[None, None, :]
    )
    weight = offset_taper(offsets)[:, None, None]
    cosine, sine = weight * np.cos(theta), weight * np.sin(theta)
    shape = (-1, PAIRS, NT // LANES, LANES)
    cosine = np.concatenate([cosine, cosine], axis=2).reshape(shape)
    sine = np.concatenate([sine, -sine], axis=2).reshape(shape)[1:]
    return cosine.astype(np.float32), sine.astype(np.float32)


def store_spectra(traces, high_ref, low_ref, spec_ref):
    quarter = high_ref.shape[0]
    parts = high_ref.shape[1] // LANES
    half = parts // 2
    rows = traces.shape[0]
    folded = jnp.concatenate([traces[:, q * quarter : (q + 1) * quarter] for q in range(4)], axis=0)
    turn = lax.broadcasted_iota(jnp.int32, (rows, LANES), 1) % 4
    odd = turn % 2 == 1
    flip_real = turn >= 2
    flip_imag = (turn == 1) | (turn == 2)
    product = jnp.dot(folded, high_ref[...], preferred_element_type=F32) + jnp.dot(
        folded, low_ref[...], preferred_element_type=F32
    )

    def turned(first, part):
        lanes = slice(part * LANES, (part + 1) * LANES)
        early = product[first * rows : (first + 1) * rows, lanes]
        late = product[(first + 2) * rows : (first + 3) * rows, lanes]
        return early + jnp.where(odd, -late, late)

    for part in range(half):
        real, imag = turned(1, part), turned(1, half + part)
        add_real, add_imag = jnp.where(odd, imag, real), jnp.where(odd, real, imag)
        spec_ref[pl.ds(part, rows, stride=parts), :] = turned(0, part) + jnp.where(
            flip_real, -add_real, add_real
        )
        spec_ref[pl.ds(half + part, rows, stride=parts), :] = turned(0, half + part) + jnp.where(
            flip_imag, -add_imag, add_imag
        )


def spectra_stage(own_hbm, high_hbm, low_hbm, spec_ref, high_ref, low_ref, own_ref, sems):
    pairs = [(own_hbm, own_ref), (high_hbm, high_ref), (low_hbm, low_ref)]
    copies = [pltpu.make_async_copy(src, dst, sems.at[i]) for i, (src, dst) in enumerate(pairs)]
    for copy in copies:
        copy.start()
    for copy in copies:
        copy.wait()
    store_spectra(own_ref[...], high_ref, low_ref, spec_ref)


def beams_stage(
    centre_hbm, count_hbm, cos_hbm, sin_hbm, own_spec_ref, within_ref, across_ref, high_ref, low_ref,
    out_ref, edge_ref, spec_ref, turned_ref, centre_ref, count_ref, cos_ref, sin_ref, sems,
):
    parts = cos_ref.shape[2]
    copies = [
        pltpu.make_async_copy(centre_hbm, centre_ref, sems.at[0]),
        pltpu.make_async_copy(count_hbm, count_ref, sems.at[1]),
        pltpu.make_async_copy(cos_hbm, cos_ref, sems.at[2]),
        pltpu.make_async_copy(sin_hbm, sin_ref, sems.at[3]),
    ]
    for copy in copies:
        copy.start()
    tile = lax.axis_index("mid")
    at_end = (tile == 0) | (tile == lax.axis_size("mid") - 1)
    within = within_ref[...].astype(F32)
    across = jnp.where(at_end, 0.0, across_ref[...].astype(F32))
    odd_tile = tile % 2 == 1
    above = jnp.where(odd_tile, within, across).astype(BF16)
    below = jnp.where(odd_tile, across, within).astype(BF16)
    edge = HALF * parts
    inner = own_spec_ref.shape[0]
    store_spectra(jnp.concatenate([above, below], axis=0), high_ref, low_ref, edge_ref)
    spec_ref[:edge] = edge_ref[:edge]
    spec_ref[edge : edge + inner] = own_spec_ref[...]
    spec_ref[edge + inner :] = edge_ref[edge:]
    for copy in copies:
        copy.wait()
    count = count_ref[tile]

    def row(index):
        return spec_ref[pl.ds(pl.multiple_of(index * parts, parts), parts), :]

    def one_beam(beam, carry):
        middle = centre_ref[beam] + HALF
        block = pl.ds(pl.multiple_of(beam * parts, parts), parts)

        @pl.when(beam < count)
        def _():
            centre = row(middle)
            even = [cos_ref[0, j] * centre for j in range(PAIRS)]
            odd_sum = [jnp.zeros_like(centre) for _ in range(PAIRS)]
            for x in range(1, HALF + 1):
                up, down = row(middle + x), row(middle - x)
                both = up + down
                swapped = pltpu.roll(up - down, parts // 2, 0)
                for j in range(PAIRS):
                    even[j] = even[j] + cos_ref[x, j] * both
                    odd_sum[j] = odd_sum[j] + sin_ref[x - 1, j] * swapped
            for j in range(PAIRS):
                turned_ref[j, block, :] = even[j] + odd_sum[j]
                turned_ref[P_SIZE - 1 - j, block, :] = even[j] - odd_sum[j]

        @pl.when(beam >= count)
        def _():
            for j in range(P_SIZE):
                turned_ref[j, block, :] = jnp.zeros((parts, LANES), F32)

        return carry

    lax.fori_loop(0, CB_DEV, one_beam, 0)
    for slope in range(P_SIZE):
        for part in range(parts):
            lanes = slice(part * LANES, (part + 1) * LANES)
            out_ref[slope, :, lanes] = turned_ref[slope, pl.ds(part, CB_DEV, stride=parts), :].astype(BF16)


def image_stage(place_ref, start_ref, beams_ref, operator_hbm, out_ref, operator_ref, sems, *, scale, copies):
    live = start_ref.shape[1]
    padded = place_ref.shape[1]
    groups, _, width = operator_ref.shape
    centres = out_ref.shape[0] * out_ref.shape[2]
    pieces = [
        pltpu.make_async_copy(
            operator_hbm.at[:, pl.ds(i * width, width)], operator_ref.at[i], sems.at[i]
        )
        for i in range(groups)
    ]
    for piece in pieces:
        piece.start()
    pick = (lax.broadcasted_iota(jnp.int32, (live, padded), 0) == place_ref[...]).astype(F32).astype(BF16)
    chosen = jnp.dot(pick, beams_ref[...], preferred_element_type=F32).astype(BF16)
    point = lax.broadcasted_iota(jnp.int32, (centres, live), 0) - start_ref[...]
    image = jnp.zeros((centres, DEPTH), F32)
    for group in range(groups):
        pieces[group].wait()
        for step in range(width // DEPTH):
            footprint = jnp.dot(
                chosen, operator_ref[group, :, step * DEPTH : (step + 1) * DEPTH], preferred_element_type=F32
            )
            high, low = split_bf16(footprint)
            hit = (point == group * (width // DEPTH) + step).astype(F32).astype(BF16)
            image = image + jnp.dot(
                jnp.concatenate([hit, hit], axis=1),
                jnp.concatenate([high, low], axis=0),
                preferred_element_type=F32,
            )
    image = (image * scale).astype(BF16)
    tile = out_ref.shape[2]
    for owner in range(out_ref.shape[0]):
        for copy in range(copies):
            out_ref[owner, copy] = image[owner * tile : (owner + 1) * tile]


VMEM = pl.BlockSpec(memory_space=pltpu.VMEM)
HBM = pl.BlockSpec(memory_space=pltpu.HBM)


def limit(mebibytes):
    return pltpu.CompilerParams(vmem_limit_bytes=mebibytes * 1024 * 1024)


def cost(flops, moved):
    return pl.CostEstimate(flops=flops, bytes_accessed=moved, transcendentals=0)


def in_hbm(array):
    return pltpu.with_memory_space_constraint(jnp.asarray(array), pltpu.HBM)


def shift(cells, axis, step):
    count = lax.axis_size(axis)
    return lax.ppermute(cells, axis, [(i, i + step) for i in range(count) if 0 <= i + step < count])


def beams_split_time(own, centre_offset, live_here):
    high = lax.Precision.HIGHEST
    sub_index = lax.axis_index("sub")
    samples = own.shape[1]
    freq_block = samples // 2
    sample_index = sub_index * samples + jnp.arange(samples, dtype=jnp.int32)[:, None]
    column = jnp.arange(NT, dtype=jnp.int32)[None, :]
    within = column % (2 * freq_block)
    frequency = column // (2 * freq_block) * freq_block + within % freq_block
    angle = 2.0 * math.pi / NT * (sample_index * frequency % NT).astype(F32)
    table = jnp.where(within // freq_block == 1, -jnp.sin(angle), jnp.cos(angle)) / math.sqrt(NT)
    partial_value = jnp.dot(own.astype(F32), table, precision=high)
    spectrum = lax.psum_scatter(partial_value, "sub", scatter_dimension=1, tiled=True)
    above = shift(spectrum[spectrum.shape[0] - HALF :], "mid", 1)
    below = shift(spectrum[:HALF], "mid", -1)
    padded = jnp.concatenate([above, spectrum, below], axis=0)
    windows = padded[centre_offset[:, None] + jnp.arange(2 * HALF + 1, dtype=jnp.int32)[None, :]]
    real, imag = windows[:, :, :freq_block], windows[:, :, freq_block:]
    offsets = np.arange(-HALF, HALF + 1)
    taper = jnp.asarray(offset_taper(offsets).astype(np.float32))[None, :, None]
    slopes = (0.25 * (np.arange(P_SIZE) - 0.5 * (P_SIZE - 1))).astype(np.float32)
    own_freq = (sub_index * freq_block + jnp.arange(freq_block, dtype=jnp.int32)).astype(F32)
    scale = (2.0 * math.pi / NT * slopes[:, None, None] * offsets[None, :, None]).astype(np.float32)
    theta = scale * own_freq[None, None, :]
    cosine, sine = taper * jnp.cos(theta), taper * jnp.sin(theta)
    add = functools.partial(jnp.einsum, "pxf,bxf->pbf", precision=high)
    beams = jnp.concatenate([add(cosine, real) + add(sine, imag), add(cosine, imag) - add(sine, real)], axis=2)
    alive = jnp.arange(CB_DEV, dtype=jnp.int32) < live_here
    return jnp.where(alive[None, :, None], beams, 0.0).astype(BF16)


def shards(traces, centre_offset, foot_start, beam_count, operator):
    mid_count = lax.axis_size("mid")
    off_count = lax.axis_size("off")
    sub_count = lax.axis_size("sub")
    mid_index = lax.axis_index("mid")
    samples = traces.shape[2]
    own = traces[0]
    counts = beam_count.astype(jnp.int32)
    tiles = jnp.arange(mid_count, dtype=jnp.int32)
    if sub_count == 1:
        odd_tile = mid_index % 2 == 1
        head, tail = own[:HALF], own[own.shape[0] - HALF :]
        ends = [(0, 0), (mid_count - 1, mid_count - 1)]
        inner_pairs = [(i, i - 1 if i % 2 == 0 else i + 1) for i in range(1, mid_count - 1)]
        within = lax.ppermute(jnp.where(odd_tile, head, tail), "mid", [(i, i ^ 1) for i in range(mid_count)])
        across = lax.ppermute(jnp.where(odd_tile, tail, head), "mid", ends + inner_pairs)
        table = quarter_table()
        slant = slant_tables()
        parts = samples // LANES
        inner = own.shape[0] * parts
        edge = 2 * HALF * parts
        spec, high, low = pl.pallas_call(
            spectra_stage,
            out_shape=[pltpu.VMEM((inner, LANES), F32)] + [pltpu.VMEM(t.shape, t.dtype) for t in table],
            in_specs=[HBM] * 3,
            out_specs=[VMEM] * 3,
            scratch_shapes=[pltpu.VMEM(own.shape, BF16), pltpu.SemaphoreType.DMA((3,))],
            compiler_params=limit(16),
            cost_estimate=cost(4 * 10**9, 4 * 10**6),
            name="spectra",
        )(in_hbm(own), *(in_hbm(t) for t in table))
        beams = pl.pallas_call(
            beams_stage,
            out_shape=pltpu.VMEM((P_SIZE, CB_DEV, samples), BF16),
            in_specs=[HBM] * 4 + [VMEM] * 5,
            out_specs=VMEM,
            scratch_shapes=[
                pltpu.VMEM((edge, LANES), F32),
                pltpu.VMEM((edge + inner, LANES), F32),
                pltpu.VMEM((P_SIZE, CB_DEV * parts, LANES), F32),
                pltpu.SMEM(centre_offset.shape, jnp.int32),
                pltpu.SMEM(beam_count.shape, jnp.int32),
            ]
            + [pltpu.VMEM(t.shape, t.dtype) for t in slant]
            + [pltpu.SemaphoreType.DMA((4,))],
            compiler_params=limit(16),
            cost_estimate=cost(4 * 10**9, 4 * 10**6),
            name="beams",
        )(in_hbm(centre_offset), in_hbm(counts), *(in_hbm(t) for t in slant), spec, within, across, high, low)
    else:
        live_here = jnp.sum(jnp.where(tiles == mid_index, counts, 0))
        beams = beams_split_time(own, centre_offset, live_here)
    shares = mid_count // P_SIZE
    if shares > 1:
        beams = jnp.repeat(beams, shares, axis=0)
    received = lax.all_to_all(
        beams.reshape(mid_count * CB_DEV, samples), "mid", split_axis=0, concat_axis=0, tiled=True
    )
    columns = operator.shape[1]
    footprint_size = FL * DEPTH
    first_column = mid_index * columns
    slope = first_column // footprint_size
    lateral_first = first_column % footprint_size // DEPTH
    rows = mid_count * CB_DEV
    live_total = rows // 2
    before = jnp.sum(jnp.where(tiles[None, :] < tiles[:, None], counts[None, :], 0), axis=1)
    slot = jnp.arange(CB_DEV, dtype=jnp.int32)
    place = jnp.where(slot[None, :] < counts[:, None], before[:, None] + slot[None, :], -1).reshape(1, rows)
    starts = lax.dynamic_index_in_dim(foot_start, slope, 1, keepdims=False)
    position = jnp.arange(live_total, dtype=jnp.int32)
    live_starts = jnp.sum(
        jnp.where(place.reshape(rows, 1) == position[None, :], starts[:, None], 0), axis=0
    )
    live_starts = (live_starts + lateral_first).reshape(1, live_total)
    partial_image = pl.pallas_call(
        functools.partial(image_stage, scale=1.0 / math.sqrt(FL * P_SIZE), copies=off_count),
        out_shape=jax.ShapeDtypeStruct((mid_count, off_count, CB_DEV, DEPTH), BF16),
        in_specs=[VMEM] * 3 + [HBM],
        out_specs=VMEM,
        scratch_shapes=[
            pltpu.VMEM((GROUPS, samples, columns // GROUPS), BF16),
            pltpu.SemaphoreType.DMA((GROUPS,)),
        ],
        compiler_params=limit(24),
        cost_estimate=cost(2 * 10**9, 10**7),
        name="image",
    )(place, live_starts, received, in_hbm(operator))
    parts = lax.all_to_all(
        partial_image.reshape(mid_count * off_count * CB_DEV, DEPTH),
        ("mid", "off"),
        split_axis=0,
        concat_axis=0,
        tiled=True,
    )
    image = jnp.sum(parts.reshape(mid_count * off_count, CB_DEV, DEPTH).astype(F32), axis=0)
    if sub_count > 1:
        image = lax.psum(image, "sub")
    return image


def solution(mesh):
    return jax.shard_map(
        shards,
        mesh=mesh,
        in_specs=(
            P("off", ("grp", "mid"), "sub"),
            P(("grp", "mid")),
            P("grp", None),
            P("grp"),
            P("sub", "mid"),
        ),
        out_specs=P(("grp", "mid"), None),
        check_vma=False,
    )
```

time: 304 us -> 52 us (0.17)
  matrix products: 150 us -> 0 us
  waiting for transfers between devices: 67.9 us -> 13.7 us
  local copies, waits for them, and re-layouts: 26.1 us -> 0.18 us
  other arithmetic: 21.8 us -> 1.79 us
  between operations: 14.4 us -> 0.11 us
  Pallas kernels: 0 us -> 9.13 us
  blocking collectives: 9.37 us -> 14.6 us
    dot_general x13 -> x0, matrix products: 150 us -> none  [the longest x8 36.7 us: add_block(): jnp.einsum('rsk,ksc->rsc', block_beams, kernels, preferred_element_type=j...]
    reduce_scatter x1 -> x0, waiting for transfers between devices: 55.4 us -> none  [shards(): lax.psum_scatter(partial_image, 'mid', scatter_dimension=0, tiled=True)]
    scatter-add x8 -> x0, other arithmetic: 16.6 us -> none  [add_block(): return partial_image.at[target].add(footprint.reshape(-1, DEPTH))]
    all_to_all x0 -> x1, blocking collectives: none -> 14.6 us  [shards(): lax.all_to_all(partial_image.reshape(mid_count * off_count * CB_DEV, DEPT...]
    psum x1 -> x0, blocking collectives: 9.37 us -> none  [shards(): image_tile = lax.psum(tile_part, ('off', 'sub'))]
    pallas_call x0 -> x3, Pallas kernels: none -> 9.13 us  [the longest x1 4.51 us: shards(): pl.pallas_call(functools.partial(image_stage, scale=1.0 / math.sqrt(FL *...]
    unnamed x14 -> x4, local copies, waits for them, and re-layouts: 9.09 us -> 0.01 us
    gather x4 -> x0, local copies, waits for them, and re-layouts: 6.25 us -> none  [the longest x2 4.12 us: shards(): windows = padded[window_index]]
  transfers between devices with their start and end apart: 4 -> 3, of which waited for: 3 -> 1; matrix products, arithmetic and copies ran while one was open for 1% -> 1% of each run, Pallas kernels for 0% -> 3%
where the time goes in v1:
time: 52 us; the launch traced here: 51.7 us
  blocking collectives  14.6 us (28%)
  waiting for transfers between devices  13.7 us (26%)
  starting transfers between devices  12.2 us (23%)
  Pallas kernels  9.13 us (18%)
  other arithmetic  1.79 us (3%)
    all_to_all x1, blocking collectives, shards(): lax.all_to_all(partial_image.reshape(mid_count * off_count * CB_DEV, DEPT...  14.6 us
    all_to_all x1, waiting for transfers between devices, shards(): lax.all_to_all(beams.reshape(mid_count * CB_DEV, samples), 'mid', split_a...  13.7 us
    all_to_all x1, starting transfers between devices, shards(): lax.all_to_all(beams.reshape(mid_count * CB_DEV, samples), 'mid', split_a...  11 us
    pallas_call x1, Pallas kernels, shards(): pl.pallas_call(functools.partial(image_stage, scale=1.0 / math.sqrt(FL *...  4.51 us
    pallas_call x1, Pallas kernels, shards(): pl.pallas_call(beams_stage, out_shape=pltpu.VMEM((P_SIZE, CB_DEV, samples...  2.83 us
    pallas_call x1, Pallas kernels, shards(): pl.pallas_call(spectra_stage, out_shape=[pltpu.VMEM((inner, LANES), F32)]...  1.79 us
  transfers between devices with their start and end apart: 3, of which 1 were waited for; matrix products, arithmetic and copies ran while one was open for 1% of the time, Pallas kernels for 3%

profile of v1, /device:TPU:0, one launch (start us, length us, event | category | flops | bytes accessed | tf_op | source)
XLA Modules:
  0.0 51.7 jit_solution(8679447593859165914)
XLA Ops:
  0.0 0.0 copy-start
  0.0 0.8 %select_bitcast_fusion = (bf16[16,1024]{1,0:T(8,128)(2,1)S(1)}, bf16[16,1024]{1,0:T(8,128)(2,1)S(1)}) fusion(pred[]{:T(512)S(6)} %eq.22, bf16[1,64,1024]{2,1,0:T(8,128)(2,1)} %param.9), kind=kLoop, calls=%fused_computation.3 | loop fusion | flops 32768 | bytes 131073 | tf_op jit(solution)/shard_map/jit(_where)/select_n | solution.py:269
  0.8 0.5 %collective-permute-start = (bf16[16,1024]{1,0:T(8,128)(2,1)S(1)}, bf16[16,1024]{1,0:T(8,128)(2,1)S(1)}, u32[]{:S(2)}, u32[]{:S(2)}) collective-permute-start(bf16[16,1024]{1,0:T(8,128)(2,1)S(1)} %get-tuple-element.12), channel_id=1, source_target_pairs={{0,2},{2,0},{4,6},{6,4},{8,10},{10,8},{12,14},{14,12},{16,18},{18,... | collective-permute-start | bytes 98312 | tf_op jit(solution)/shard_map/ppermute | solution.py:268
  1.3 0.7 %collective-permute-start.1 = (bf16[16,1024]{1,0:T(8,128)(2,1)S(1)}, bf16[16,1024]{1,0:T(8,128)(2,1)S(1)}, u32[]{:S(2)}, u32[]{:S(2)}) collective-permute-start(bf16[16,1024]{1,0:T(8,128)(2,1)S(1)} %get-tuple-element.11), channel_id=1, source_target_pairs={{0,0},{30,30},{2,4},{4,2},{6,8},{8,6},{10,12},{12,10},{14,16},{16,... | collective-permute-start | bytes 98312 | tf_op jit(solution)/shard_map/ppermute | solution.py:269
  2.0 1.8 %spectra.1 = (f32[512,128]{1,0:T(8,128)S(1)}, bf16[256,1024]{1,0:T(8,128)(2,1)S(1)}, bf16[256,1024]{1,0:T(8,128)(2,1)S(1)}) custom-call(bf16[64,1024]{1,0:T(8,128)(2,1)} %bitcast.12, bf16[256,1024]{1,0:T(8,128)(2,1)} %constant.70.clone.high_hbm, bf16[256,1024]{1,0:T(8,128)(2,1)} %constant.71.clone.low_hbm), custom_call_target="tpu_custom_call" | custom-call | flops 4000000000 | bytes 4000000 | tf_op jit(solution)/shard_map/spectra/pallas_call | solution.py:275
  3.8 0.0 copy-start.1
  3.8 0.0 collective-permute-done.within_ref
  3.8 0.0 collective-permute-done.1.across_ref
  3.8 2.8 %beams.1 = bf16[16,16,1024]{2,1,0:T(8,128)(2,1)} custom-call(s32[16]{0:T(128)} %centre_hbm.1, s32[16]{0:T(128)} %count_hbm.1, f32[17,8,8,128]{3,2,1,0:T(8,128)} %constant.72.clone.cos_hbm, f32[16,8,8,128]{3,2,1,0:T(8,128)} %constant.73.clone.sin_hbm, f32[512,128]{1,0:T(8,128)S(1)} %get-tuple-element.8.own_spec_ref, ...), custom_call_target="tpu_custom_call" | custom-call | flops 4000000000 | bytes 4000000 | tf_op jit(solution)/shard_map/beams/pallas_call | solution.py:285
  6.7 11.0 %all-to-all-start = ((bf16[16,16,1024]{2,1,0:T(8,128)(2,1)}), bf16[16,16,1024]{2,1,0:T(8,128)(2,1)S(1)}, u32[]{:S(2)}, u32[]{:S(2)}) async-start(bf16[16,16,1024]{2,1,0:T(8,128)(2,1)} %beams.1), calls=%async_computation | async-start | bytes 1048576 | tf_op jit(solution)/shard_map/all_to_all | solution.py:309
  17.7 0.0 copy-done.1
  17.7 0.1 select_reduce_fusion.1
  17.8 0.1 add_select_fusion
  17.9 0.1 select_n.72
  18.0 0.1 select_n.71.place_ref
  18.1 0.0 copy-done
  18.1 0.1 select_reduce_fusion
  18.2 13.7 %all-to-all-done = bf16[16,16,1024]{2,1,0:T(8,128)(2,1)S(1)} async-done(((bf16[16,16,1024]{2,1,0:T(8,128)(2,1)}), bf16[16,16,1024]{2,1,0:T(8,128)(2,1)S(1)}, u32[]{:S(2)}, u32[]{:S(2)}) %all-to-all-start) | async-done | bytes 524320 | tf_op jit(solution)/shard_map/all_to_all | solution.py:309
  31.9 4.5 %image.1 = bf16[16,2,16,256]{3,2,1,0:T(8,128)(2,1)S(1)} custom-call(s32[1,256]{1,0:T(1,128)S(1)} %select_n.71.place_ref, s32[1,128]{1,0:T(1,128)S(1)} %add_bitcast_fusion.start_ref, bf16[256,1024]{1,0:T(8,128)(2,1)S(1)} %bitcast.10, bf16[1024,4096]{1,0:T(8,128)(2,1)} %operator_hbm.1), custom_call_target="tpu_custom_call" | custom-call | flops 2000000000 | bytes 10000000 | tf_op jit(solution)/shard_map/image/pallas_call | solution.py:328
  36.5 14.6 %all_to_all.17 = bf16[32,16,256]{2,1,0:T(8,128)(2,1)S(1)} all-to-all(bf16[32,16,256]{2,1,0:T(8,128)(2,1)S(1)} %bitcast.11), channel_id=1, replica_groups=mesh['grp'=1,'mid'=16,'off'=2,'sub'=1] {'mid','off'}, dimensions={0} | all-to-all | bytes 524288 | tf_op jit(solution)/shard_map/all_to_all | solution.py:341
  51.0 0.7 %convert_reduce_fusion = f32[16,256]{1,0:T(8,128)} fusion(bf16[32,16,256]{2,1,0:T(8,128)(2,1)S(1)} %all_to_all.17), kind=kLoop, calls=%fused_computation | loop fusion | flops 258048 | bytes 278528 | tf_op jit(solution)/shard_map/reduce_sum | solution.py:348
  (2 shorter events, 0.0 us)
Async XLA Ops:
  0.0 18.1 %copy-start = (s32[256,16]{0,1:T(8,128)S(1)}, s32[256,16]{0,1:T(8,128)}, u32[]{:S(2)}) copy-start(s32[256,16]{0,1:T(8,128)} %param.11) | copy-start | bytes 49156
  0.8 3.0 %collective-permute-start = (bf16[16,1024]{1,0:T(8,128)(2,1)S(1)}, bf16[16,1024]{1,0:T(8,128)(2,1)S(1)}, u32[]{:S(2)}, u32[]{:S(2)}) collective-permute-start(bf16[16,1024]{1,0:T(8,128)(2,1)S(1)} %get-tuple-element.12), channel_id=1, source_target_pairs={{0,2},{2,0},{4,6},{6,4},{8,10},{10,8},{12,14},{14,12},{16,18},{18,... | collective-permute-start | bytes 98312 | tf_op jit(solution)/shard_map/ppermute | solution.py:268
  1.3 2.5 %collective-permute-start.1 = (bf16[16,1024]{1,0:T(8,128)(2,1)S(1)}, bf16[16,1024]{1,0:T(8,128)(2,1)S(1)}, u32[]{:S(2)}, u32[]{:S(2)}) collective-permute-start(bf16[16,1024]{1,0:T(8,128)(2,1)S(1)} %get-tuple-element.11), channel_id=1, source_target_pairs={{0,0},{30,30},{2,4},{4,2},{6,8},{8,6},{10,12},{12,10},{14,16},{16,... | collective-permute-start | bytes 98312 | tf_op jit(solution)/shard_map/ppermute | solution.py:269
  3.8 13.9 %copy-start.1 = (s32[16]{0:T(128)S(1)}, s32[16]{0:T(128)}, u32[]{:S(2)}) copy-start(s32[16]{0:T(128)} %count_hbm.1) | copy-start | bytes 196
  6.7 25.3 %all-to-all-start = ((bf16[16,16,1024]{2,1,0:T(8,128)(2,1)}), bf16[16,16,1024]{2,1,0:T(8,128)(2,1)S(1)}, u32[]{:S(2)}, u32[]{:S(2)}) async-start(bf16[16,16,1024]{2,1,0:T(8,128)(2,1)} %beams.1), calls=%async_computation | async-start | bytes 1048576 | tf_op jit(solution)/shard_map/all_to_all | solution.py:309

commit v2 on v1

--- a/solution.py
+++ b/solution.py
@@ -17,7 +17,7 @@
 CB_DEV = 16
 PAIRS = P_SIZE // 2
 LANES = 128
-GROUPS = 4
+PIECES = 4
 BF16 = jnp.bfloat16
 F32 = jnp.float32
 
@@ -85,27 +85,65 @@
         )
 
 
-def spectra_stage(own_hbm, high_hbm, low_hbm, spec_ref, high_ref, low_ref, own_ref, sems):
-    pairs = [(own_hbm, own_ref), (high_hbm, high_ref), (low_hbm, low_ref)]
+def live_layout(counts, starts, live):
+    padded = starts.shape[1]
+    beam = lax.broadcasted_iota(jnp.int32, (1, padded), 1)
+    place = jnp.full((1, padded), -1, jnp.int32)
+    before = jnp.int32(0)
+    for tile in range(padded // CB_DEV):
+        slot = beam - tile * CB_DEV
+        here = (slot >= 0) & (slot < counts[tile])
+        place = jnp.where(here, before + slot, place)
+        before = before + counts[tile]
+    pick = (lax.broadcasted_iota(jnp.int32, (live, padded), 0) == place).astype(F32).astype(BF16)
+    row = lax.broadcasted_iota(jnp.int32, (8, padded), 0)
+    digits = jnp.where(row == 0, starts % CB_DEV, jnp.where(row == 1, starts // CB_DEV, 0))
+    digits = lax.dot_general(
+        digits.astype(F32).astype(BF16), pick, (((1,), (1,)), ((), ())), preferred_element_type=F32
+    )
+    return place, (digits[0:1] + CB_DEV * digits[1:2]).astype(jnp.int32)
+
+
+def half_columns(operator_hbm, held_ref, half):
+    depth, width = held_ref.shape[0] // PIECES, held_ref.shape[1]
+    blocks = [pl.ds(piece * depth, depth) for piece in range(PIECES)]
+    return [(operator_hbm.at[rows, pl.ds(half * width, width)], held_ref.at[rows]) for rows in blocks]
+
+
+def first_stage(
+    own_hbm, high_hbm, low_hbm, count_hbm, point_hbm, cos_hbm, sin_hbm, operator_hbm,
+    spec_ref, high_ref, low_ref, cos_ref, sin_ref, operator_ref, place_ref, start_ref,
+    own_ref, count_ref, point_ref, sems,
+):
+    pairs = [
+        (own_hbm, own_ref), (high_hbm, high_ref), (low_hbm, low_ref), (count_hbm, count_ref),
+        (point_hbm, point_ref), (cos_hbm, cos_ref), (sin_hbm, sin_ref),
+    ]
+    pairs += half_columns(operator_hbm, operator_ref, 0)
     copies = [pltpu.make_async_copy(src, dst, sems.at[i]) for i, (src, dst) in enumerate(pairs)]
     for copy in copies:
         copy.start()
-    for copy in copies:
+    for copy in copies[:5]:
         copy.wait()
     store_spectra(own_ref[...], high_ref, low_ref, spec_ref)
+    first_column = lax.axis_index("mid") * operator_hbm.shape[1]
+    slope = first_column // (FL * DEPTH)
+    rows = lax.broadcasted_iota(jnp.int32, point_ref.shape, 0)
+    starts = jnp.sum(jnp.where(rows == slope, point_ref[...], 0), axis=0, keepdims=True)
+    place, live_starts = live_layout(count_ref, starts, start_ref.shape[1])
+    place_ref[...] = place
+    start_ref[...] = live_starts + first_column % (FL * DEPTH) // DEPTH
+    for copy in copies[5:]:
+        copy.wait()
 
 
 def beams_stage(
-    centre_hbm, count_hbm, cos_hbm, sin_hbm, own_spec_ref, within_ref, across_ref, high_ref, low_ref,
-    out_ref, edge_ref, spec_ref, turned_ref, centre_ref, count_ref, cos_ref, sin_ref, sems,
+    centre_hbm, count_hbm, operator_hbm, own_spec_ref, within_ref, across_ref, high_ref, low_ref, cos_ref, sin_ref,
+    out_ref, held_ref, edge_ref, spec_ref, turned_ref, centre_ref, count_ref, sems,
 ):
     parts = cos_ref.shape[2]
-    copies = [
-        pltpu.make_async_copy(centre_hbm, centre_ref, sems.at[0]),
-        pltpu.make_async_copy(count_hbm, count_ref, sems.at[1]),
-        pltpu.make_async_copy(cos_hbm, cos_ref, sems.at[2]),
-        pltpu.make_async_copy(sin_hbm, sin_ref, sems.at[3]),
-    ]
+    pairs = [(centre_hbm, centre_ref), (count_hbm, count_ref)] + half_columns(operator_hbm, held_ref, 1)
+    copies = [pltpu.make_async_copy(src, dst, sems.at[i]) for i, (src, dst) in enumerate(pairs)]
     for copy in copies:
         copy.start()
     tile = lax.axis_index("mid")
@@ -121,7 +159,7 @@
     spec_ref[:edge] = edge_ref[:edge]
     spec_ref[edge : edge + inner] = own_spec_ref[...]
     spec_ref[edge + inner :] = edge_ref[edge:]
-    for copy in copies:
+    for copy in copies[:2]:
         copy.wait()
     count = count_ref[tile]
 
@@ -160,38 +198,30 @@
         for part in range(parts):
             lanes = slice(part * LANES, (part + 1) * LANES)
             out_ref[slope, :, lanes] = turned_ref[slope, pl.ds(part, CB_DEV, stride=parts), :].astype(BF16)
-
-
-def image_stage(place_ref, start_ref, beams_ref, operator_hbm, out_ref, operator_ref, sems, *, scale, copies):
+    for copy in copies[2:]:
+        copy.wait()
+
+
+def image_stage(place_ref, start_ref, beams_ref, early_ref, late_ref, out_ref, *, scale, copies):
     live = start_ref.shape[1]
     padded = place_ref.shape[1]
-    groups, _, width = operator_ref.shape
+    half = early_ref.shape[1] // DEPTH
     centres = out_ref.shape[0] * out_ref.shape[2]
-    pieces = [
-        pltpu.make_async_copy(
-            operator_hbm.at[:, pl.ds(i * width, width)], operator_ref.at[i], sems.at[i]
-        )
-        for i in range(groups)
-    ]
-    for piece in pieces:
-        piece.start()
     pick = (lax.broadcasted_iota(jnp.int32, (live, padded), 0) == place_ref[...]).astype(F32).astype(BF16)
     chosen = jnp.dot(pick, beams_ref[...], preferred_element_type=F32).astype(BF16)
     point = lax.broadcasted_iota(jnp.int32, (centres, live), 0) - start_ref[...]
     image = jnp.zeros((centres, DEPTH), F32)
-    for group in range(groups):
-        pieces[group].wait()
-        for step in range(width // DEPTH):
-            footprint = jnp.dot(
-                chosen, operator_ref[group, :, step * DEPTH : (step + 1) * DEPTH], preferred_element_type=F32
-            )
-            high, low = split_bf16(footprint)
-            hit = (point == group * (width // DEPTH) + step).astype(F32).astype(BF16)
-            image = image + jnp.dot(
-                jnp.concatenate([hit, hit], axis=1),
-                jnp.concatenate([high, low], axis=0),
-                preferred_element_type=F32,
-            )
+    for step in range(2 * half):
+        columns = slice(step % half * DEPTH, (step % half + 1) * DEPTH)
+        operator_ref = early_ref if step < half else late_ref
+        footprint = jnp.dot(chosen, operator_ref[:, columns], preferred_element_type=F32)
+        high, low = split_bf16(footprint)
+        hit = (point == step).astype(F32).astype(BF16)
+        image = image + jnp.dot(
+            jnp.concatenate([hit, hit], axis=1),
+            jnp.concatenate([high, low], axis=0),
+            preferred_element_type=F32,
+        )
     image = (image * scale).astype(BF16)
     tile = out_ref.shape[2]
     for owner in range(out_ref.shape[0]):
@@ -260,6 +290,8 @@
     own = traces[0]
     counts = beam_count.astype(jnp.int32)
     tiles = jnp.arange(mid_count, dtype=jnp.int32)
+    rows = mid_count * CB_DEV
+    live_total = rows // 2
     if sub_count == 1:
         odd_tile = mid_index % 2 == 1
         head, tail = own[:HALF], own[own.shape[0] - HALF :]
@@ -267,77 +299,74 @@
         inner_pairs = [(i, i - 1 if i % 2 == 0 else i + 1) for i in range(1, mid_count - 1)]
         within = lax.ppermute(jnp.where(odd_tile, head, tail), "mid", [(i, i ^ 1) for i in range(mid_count)])
         across = lax.ppermute(jnp.where(odd_tile, tail, head), "mid", ends + inner_pairs)
-        table = quarter_table()
-        slant = slant_tables()
+        tables = quarter_table() + slant_tables()
         parts = samples // LANES
         inner = own.shape[0] * parts
         edge = 2 * HALF * parts
-        spec, high, low = pl.pallas_call(
-            spectra_stage,
-            out_shape=[pltpu.VMEM((inner, LANES), F32)] + [pltpu.VMEM(t.shape, t.dtype) for t in table],
-            in_specs=[HBM] * 3,
-            out_specs=[VMEM] * 3,
-            scratch_shapes=[pltpu.VMEM(own.shape, BF16), pltpu.SemaphoreType.DMA((3,))],
+        half_shape = (operator.shape[0], operator.shape[1] // 2)
+        spec, high, low, cosine, sine, operator_early, place, live_starts = pl.pallas_call(
+            first_stage,
+            out_shape=[pltpu.VMEM((inner, LANES), F32)]
+            + [pltpu.VMEM(t.shape, t.dtype) for t in tables]
+            + [pltpu.VMEM(half_shape, BF16)]
+            + [pltpu.VMEM((1, n), jnp.int32) for n in (rows, live_total)],
+            in_specs=[HBM] * 8,
+            out_specs=[VMEM] * 8,
+            scratch_shapes=[
+                pltpu.VMEM(own.shape, BF16),
+                pltpu.SMEM(counts.shape, jnp.int32),
+                pltpu.VMEM((P_SIZE, rows), jnp.int32),
+                pltpu.SemaphoreType.DMA((7 + PIECES,)),
+            ],
             compiler_params=limit(16),
-            cost_estimate=cost(4 * 10**9, 4 * 10**6),
-            name="spectra",
-        )(in_hbm(own), *(in_hbm(t) for t in table))
-        beams = pl.pallas_call(
+            cost_estimate=cost(4 * 10**9, 10**7),
+            name="first",
+        )(*(in_hbm(t) for t in (own,) + tables[:2] + (counts, foot_start.T) + tables[2:] + (operator,)))
+        beams, operator_late = pl.pallas_call(
             beams_stage,
-            out_shape=pltpu.VMEM((P_SIZE, CB_DEV, samples), BF16),
-            in_specs=[HBM] * 4 + [VMEM] * 5,
-            out_specs=VMEM,
+            out_shape=[pltpu.VMEM((P_SIZE, CB_DEV, samples), BF16), pltpu.VMEM(half_shape, BF16)],
+            in_specs=[HBM] * 3 + [VMEM] * 7,
+            out_specs=[VMEM] * 2,
             scratch_shapes=[
                 pltpu.VMEM((edge, LANES), F32),
                 pltpu.VMEM((edge + inner, LANES), F32),
                 pltpu.VMEM((P_SIZE, CB_DEV * parts, LANES), F32),
                 pltpu.SMEM(centre_offset.shape, jnp.int32),
                 pltpu.SMEM(beam_count.shape, jnp.int32),
-            ]
-            + [pltpu.VMEM(t.shape, t.dtype) for t in slant]
-            + [pltpu.SemaphoreType.DMA((4,))],
+                pltpu.SemaphoreType.DMA((2 + PIECES,)),
+            ],
             compiler_params=limit(16),
             cost_estimate=cost(4 * 10**9, 4 * 10**6),
             name="beams",
-        )(in_hbm(centre_offset), in_hbm(counts), *(in_hbm(t) for t in slant), spec, within, across, high, low)
+        )(in_hbm(centre_offset), in_hbm(counts), in_hbm(operator), spec, within, across, high, low, cosine, sine)
     else:
         live_here = jnp.sum(jnp.where(tiles == mid_index, counts, 0))
         beams = beams_split_time(own, centre_offset, live_here)
+        operator_early, operator_late = jnp.split(operator, 2, axis=1)
+        first_column = mid_index * operator.shape[1]
+        before = jnp.sum(jnp.where(tiles[None, :] < tiles[:, None], counts[None, :], 0), axis=1)
+        slot = jnp.arange(CB_DEV, dtype=jnp.int32)
+        place = jnp.where(slot[None, :] < counts[:, None], before[:, None] + slot[None, :], -1).reshape(1, rows)
+        starts = lax.dynamic_index_in_dim(foot_start, first_column // (FL * DEPTH), 1, keepdims=False)
+        position = jnp.arange(live_total, dtype=jnp.int32)
+        here = place.reshape(rows, 1) == position[None, :]
+        live_starts = jnp.sum(jnp.where(here, starts[:, None], 0), axis=0)
+        live_starts = (live_starts + first_column % (FL * DEPTH) // DEPTH).reshape(1, live_total)
     shares = mid_count // P_SIZE
     if shares > 1:
         beams = jnp.repeat(beams, shares, axis=0)
     received = lax.all_to_all(
         beams.reshape(mid_count * CB_DEV, samples), "mid", split_axis=0, concat_axis=0, tiled=True
     )
-    columns = operator.shape[1]
-    footprint_size = FL * DEPTH
-    first_column = mid_index * columns
-    slope = first_column // footprint_size
-    lateral_first = first_column % footprint_size // DEPTH
-    rows = mid_count * CB_DEV
-    live_total = rows // 2
-    before = jnp.sum(jnp.where(tiles[None, :] < tiles[:, None], counts[None, :], 0), axis=1)
-    slot = jnp.arange(CB_DEV, dtype=jnp.int32)
-    place = jnp.where(slot[None, :] < counts[:, None], before[:, None] + slot[None, :], -1).reshape(1, rows)
-    starts = lax.dynamic_index_in_dim(foot_start, slope, 1, keepdims=False)
-    position = jnp.arange(live_total, dtype=jnp.int32)
-    live_starts = jnp.sum(
-        jnp.where(place.reshape(rows, 1) == position[None, :], starts[:, None], 0), axis=0
-    )
-    live_starts = (live_starts + lateral_first).reshape(1, live_total)
     partial_image = pl.pallas_call(
         functools.partial(image_stage, scale=1.0 / math.sqrt(FL * P_SIZE), copies=off_count),
         out_shape=jax.ShapeDtypeStruct((mid_count, off_count, CB_DEV, DEPTH), BF16),
-        in_specs=[VMEM] * 3 + [HBM],
+        in_specs=[VMEM] * 5,
         out_specs=VMEM,
-        scratch_shapes=[
-            pltpu.VMEM((GROUPS, samples, columns // GROUPS), BF16),
-            pltpu.SemaphoreType.DMA((GROUPS,)),
-        ],
         compiler_params=limit(24),
         cost_estimate=cost(2 * 10**9, 10**7),
         name="image",
-    )(place, live_starts, received, in_hbm(operator))
+    )(place, live_starts, received, operator_early, operator_late)
     parts = lax.all_to_all(
         partial_image.reshape(mid_count * off_count * CB_DEV, DEPTH),
         ("mid", "off"),

time: 52 us -> 48.4 us (0.931)
  blocking collectives: 14.6 us -> 33.6 us
  waiting for transfers between devices: 13.7 us -> 0.01 us
  starting transfers between devices: 12.2 us -> 5.08 us
  Pallas kernels: 9.13 us -> 7.96 us
    all_to_all x0 -> x1, blocking collectives: none -> 19 us  [shards(): lax.all_to_all(beams.reshape(mid_count * CB_DEV, samples), 'mid', split_a...]
    all_to_all x1 -> x0, waiting for transfers between devices: 13.7 us -> none  [shards(): lax.all_to_all(beams.reshape(mid_count * CB_DEV, samples), 'mid', split_a...]
    all_to_all x1 -> x0, starting transfers between devices: 11 us -> none  [shards(): lax.all_to_all(beams.reshape(mid_count * CB_DEV, samples), 'mid', split_a...]
    ppermute x1, starting transfers between devices: 0.55 us -> 4.42 us  [shards(): lax.ppermute(jnp.where(odd_tile, head, tail), 'mid', [(i, i ^ 1) for i in...]
    pallas_call x1, Pallas kernels: 4.51 us -> 2.6 us  [shards(): pl.pallas_call(functools.partial(image_stage, scale=1.0 / math.sqrt(FL *...]
    pallas_call x2, Pallas kernels: 4.62 us -> 5.36 us  [the longest x1 2.99 us: shards(): pl.pallas_call(first_stage, out_shape=[pltpu.VMEM((inner, LANES), F32)] +...]
  transfers between devices with their start and end apart: 3 -> 2, of which waited for: 1 -> 0; matrix products, arithmetic and copies ran while one was open for 1% -> 0% of each run, Pallas kernels for 3% -> 6%
where the time goes in v2:
time: 48.4 us; the launch traced here: 48.1 us
  blocking collectives  33.6 us (69%)
  Pallas kernels  7.96 us (16%)
  starting transfers between devices  5.08 us (10%)
  other arithmetic  1.43 us (3%)
    all_to_all x1, blocking collectives, shards(): lax.all_to_all(beams.reshape(mid_count * CB_DEV, samples), 'mid', split_a...  19 us
    all_to_all x1, blocking collectives, shards(): lax.all_to_all(partial_image.reshape(mid_count * off_count * CB_DEV, DEPT...  14.5 us
    ppermute x1, starting transfers between devices, shards(): lax.ppermute(jnp.where(odd_tile, head, tail), 'mid', [(i, i ^ 1) for i in...  4.42 us
    pallas_call x1, Pallas kernels, shards(): pl.pallas_call(first_stage, out_shape=[pltpu.VMEM((inner, LANES), F32)] +...  2.99 us
    pallas_call x1, Pallas kernels, shards(): pl.pallas_call(functools.partial(image_stage, scale=1.0 / math.sqrt(FL *...  2.6 us
    pallas_call x1, Pallas kernels, shards(): pl.pallas_call(beams_stage, out_shape=[pltpu.VMEM((P_SIZE, CB_DEV, sample...  2.37 us
  transfers between devices with their start and end apart: 2, of which 0 were waited for; matrix products, arithmetic and copies ran while one was open for 0% of the time, Pallas kernels for 6%

profile of v2, /device:TPU:0, one launch (start us, length us, event | category | flops | bytes accessed | tf_op | source)
XLA Modules:
  0.0 48.1 jit_solution(2079066294382302315)
XLA Ops:
  0.0 0.8 %select_bitcast_fusion = (bf16[16,1024]{1,0:T(8,128)(2,1)S(1)}, bf16[16,1024]{1,0:T(8,128)(2,1)S(1)}) fusion(pred[]{:T(512)S(6)} %eq.5, bf16[1,64,1024]{2,1,0:T(8,128)(2,1)} %param.9), kind=kLoop, calls=%fused_computation.1 | loop fusion | flops 32768 | bytes 131073 | tf_op jit(solution)/shard_map/jit(_where)/select_n | solution.py:301
  0.8 0.7 %collective-permute-start.1 = (bf16[16,1024]{1,0:T(8,128)(2,1)S(1)}, bf16[16,1024]{1,0:T(8,128)(2,1)S(1)}, u32[]{:S(2)}, u32[]{:S(2)}) collective-permute-start(bf16[16,1024]{1,0:T(8,128)(2,1)S(1)} %get-tuple-element.25), channel_id=1, source_target_pairs={{0,0},{30,30},{2,4},{4,2},{6,8},{8,6},{10,12},{12,10},{14,16},{16,... | collective-permute-start | bytes 98312 | tf_op jit(solution)/shard_map/ppermute | solution.py:301
  1.4 4.4 %collective-permute-start = (bf16[16,1024]{1,0:T(8,128)(2,1)S(1)}, bf16[16,1024]{1,0:T(8,128)(2,1)S(1)}, u32[]{:S(2)}, u32[]{:S(2)}) collective-permute-start(bf16[16,1024]{1,0:T(8,128)(2,1)S(1)} %get-tuple-element.26), channel_id=1, source_target_pairs={{0,2},{2,0},{4,6},{6,4},{8,10},{10,8},{12,14},{14,12},{16,18},{18,... | collective-permute-start | bytes 98312 | tf_op jit(solution)/shard_map/ppermute | solution.py:300
  5.9 3.0 %first.1 = (f32[512,128]{1,0:T(8,128)S(1)}, bf16[256,1024]{1,0:T(8,128)(2,1)S(1)}, bf16[256,1024]{1,0:T(8,128)(2,1)S(1)}, f32[17,8,8,128]{3,2,1,0:T(8,128)S(1)},...) custom-call(bf16[64,1024]{1,0:T(8,128)(2,1)} %bitcast.10, ...), custom_call_target="tpu_custom_call" | custom-call | flops 4000000000 | bytes 10000000 | tf_op jit(solution)/shard_map/first/pallas_call | solution.py:307
  8.9 0.0 collective-permute-done.1.across_ref
  8.9 0.0 collective-permute-done.within_ref
  8.9 2.4 %beams.1 = (bf16[16,16,1024]{2,1,0:T(8,128)(2,1)S(1)}, bf16[1024,2048]{1,0:T(8,128)(2,1)S(1)}) custom-call(s32[16]{0:T(128)} %centre_hbm.1, s32[16]{0:T(128)} %count_hbm.3, bf16[1024,4096]{1,0:T(8,128)(2,1)} %operator_hbm.3, f32[512,128]{1,0:T(8,128)S(1)} %get-tuple-element.17.own_spec_ref, bf16[16,1024]{1,0:T(8,128)(2,1)S(1)} %collective-permute-done.within_ref, ...), custom_call_target="tpu_custom_call" | custom-call | flops 4000000000 | bytes 4000000 | tf_op jit(solution)/shard_map/beams/pallas_call | solution.py:325
  11.3 19.0 %all_to_all.17 = bf16[16,16,1024]{2,1,0:T(8,128)(2,1)S(1)} all-to-all(bf16[16,16,1024]{2,1,0:T(8,128)(2,1)S(1)} %get-tuple-element.22), channel_id=1, replica_groups=mesh['grp'=1,'mid'=16,'off'=2,'sub'=1] {'mid'}, dimensions={0} | all-to-all | bytes 1048576 | tf_op jit(solution)/shard_map/all_to_all | solution.py:358
  30.3 2.6 %image.1 = bf16[16,2,16,256]{3,2,1,0:T(8,128)(2,1)S(1)} custom-call(s32[1,256]{1,0:T(1,128)S(1)} %get-tuple-element.15.place_ref, s32[1,128]{1,0:T(1,128)S(1)} %get-tuple-element.16.start_ref, bf16[256,1024]{1,0:T(8,128)(2,1)S(1)} %bitcast.8, bf16[1024,2048]{1,0:T(8,128)(2,1)S(1)} %get-tuple-element.23.early_ref, ...), custom_call_target="tpu_custom_call" | custom-call | flops 2000000000 | bytes 10000000 | tf_op jit(solution)/shard_map/image/pallas_call | solution.py:361
  32.9 14.5 %all_to_all.18 = bf16[32,16,256]{2,1,0:T(8,128)(2,1)S(1)} all-to-all(bf16[32,16,256]{2,1,0:T(8,128)(2,1)S(1)} %bitcast.9), channel_id=1, replica_groups=mesh['grp'=1,'mid'=16,'off'=2,'sub'=1] {'mid','off'}, dimensions={0} | all-to-all | bytes 524288 | tf_op jit(solution)/shard_map/all_to_all | solution.py:370
  47.5 0.7 %convert_reduce_fusion = f32[16,256]{1,0:T(8,128)} fusion(bf16[32,16,256]{2,1,0:T(8,128)(2,1)S(1)} %all_to_all.18), kind=kLoop, calls=%fused_computation | loop fusion | flops 258048 | bytes 278528 | tf_op jit(solution)/shard_map/reduce_sum | solution.py:377
Async XLA Ops:
  0.8 8.1 %collective-permute-start.1 = (bf16[16,1024]{1,0:T(8,128)(2,1)S(1)}, bf16[16,1024]{1,0:T(8,128)(2,1)S(1)}, u32[]{:S(2)}, u32[]{:S(2)}) collective-permute-start(bf16[16,1024]{1,0:T(8,128)(2,1)S(1)} %get-tuple-element.25), channel_id=1, source_target_pairs={{0,0},{30,30},{2,4},{4,2},{6,8},{8,6},{10,12},{12,10},{14,16},{16,... | collective-permute-start | bytes 98312 | tf_op jit(solution)/shard_map/ppermute | solution.py:301
  1.4 7.4 %collective-permute-start = (bf16[16,1024]{1,0:T(8,128)(2,1)S(1)}, bf16[16,1024]{1,0:T(8,128)(2,1)S(1)}, u32[]{:S(2)}, u32[]{:S(2)}) collective-permute-start(bf16[16,1024]{1,0:T(8,128)(2,1)S(1)} %get-tuple-element.26), channel_id=1, source_target_pairs={{0,2},{2,0},{4,6},{6,4},{8,10},{10,8},{12,14},{14,12},{16,18},{18,... | collective-permute-start | bytes 98312 | tf_op jit(solution)/shard_map/ppermute | solution.py:300

commit v3 on v2

--- a/solution.py
+++ b/solution.py
@@ -18,6 +18,7 @@
 PAIRS = P_SIZE // 2
 LANES = 128
 PIECES = 4
+SHARES = (3, 3)
 BF16 = jnp.bfloat16
 F32 = jnp.float32
 
@@ -104,25 +105,29 @@
     return place, (digits[0:1] + CB_DEV * digits[1:2]).astype(jnp.int32)
 
 
-def half_columns(operator_hbm, held_ref, half):
+def column_copies(operator_hbm, held_ref, first):
     depth, width = held_ref.shape[0] // PIECES, held_ref.shape[1]
     blocks = [pl.ds(piece * depth, depth) for piece in range(PIECES)]
-    return [(operator_hbm.at[rows, pl.ds(half * width, width)], held_ref.at[rows]) for rows in blocks]
+    return [(operator_hbm.at[rows, pl.ds(first, width)], held_ref.at[rows]) for rows in blocks]
+
+
+def started(pairs, sems):
+    copies = [pltpu.make_async_copy(src, dst, sems.at[i]) for i, (src, dst) in enumerate(pairs)]
+    for copy in copies:
+        copy.start()
+    return copies
 
 
 def first_stage(
-    own_hbm, high_hbm, low_hbm, count_hbm, point_hbm, cos_hbm, sin_hbm, operator_hbm,
-    spec_ref, high_ref, low_ref, cos_ref, sin_ref, operator_ref, place_ref, start_ref,
-    own_ref, count_ref, point_ref, sems,
+    own_hbm, high_hbm, low_hbm, count_hbm, point_hbm, centre_hbm, cos_hbm, sin_hbm, operator_hbm,
+    spec_ref, high_ref, low_ref, cos_ref, sin_ref, early_ref, place_ref, start_ref, count_ref, centre_ref,
+    own_ref, point_ref, sems,
 ):
     pairs = [
         (own_hbm, own_ref), (high_hbm, high_ref), (low_hbm, low_ref), (count_hbm, count_ref),
-        (point_hbm, point_ref), (cos_hbm, cos_ref), (sin_hbm, sin_ref),
+        (point_hbm, point_ref), (centre_hbm, centre_ref), (cos_hbm, cos_ref), (sin_hbm, sin_ref),
     ]
-    pairs += half_columns(operator_hbm, operator_ref, 0)
-    copies = [pltpu.make_async_copy(src, dst, sems.at[i]) for i, (src, dst) in enumerate(pairs)]
-    for copy in copies:
-        copy.start()
+    copies = started(pairs + column_copies(operator_hbm, early_ref, 0), sems)
     for copy in copies[:5]:
         copy.wait()
     store_spectra(own_ref[...], high_ref, low_ref, spec_ref)
@@ -138,14 +143,11 @@
 
 
 def beams_stage(
-    centre_hbm, count_hbm, operator_hbm, own_spec_ref, within_ref, across_ref, high_ref, low_ref, cos_ref, sin_ref,
-    out_ref, held_ref, edge_ref, spec_ref, turned_ref, centre_ref, count_ref, sems,
+    centre_ref, count_ref, operator_hbm, own_spec_ref, within_ref, across_ref, high_ref, low_ref, cos_ref, sin_ref,
+    out_ref, middle_ref, edge_ref, spec_ref, turned_ref, sems, *, first_column,
 ):
     parts = cos_ref.shape[2]
-    pairs = [(centre_hbm, centre_ref), (count_hbm, count_ref)] + half_columns(operator_hbm, held_ref, 1)
-    copies = [pltpu.make_async_copy(src, dst, sems.at[i]) for i, (src, dst) in enumerate(pairs)]
-    for copy in copies:
-        copy.start()
+    copies = started(column_copies(operator_hbm, middle_ref, first_column), sems)
     tile = lax.axis_index("mid")
     at_end = (tile == 0) | (tile == lax.axis_size("mid") - 1)
     within = within_ref[...].astype(F32)
@@ -159,8 +161,6 @@
     spec_ref[:edge] = edge_ref[:edge]
     spec_ref[edge : edge + inner] = own_spec_ref[...]
     spec_ref[edge + inner :] = edge_ref[edge:]
-    for copy in copies[:2]:
-        copy.wait()
     count = count_ref[tile]
 
     def row(index):
@@ -198,22 +198,29 @@
         for part in range(parts):
             lanes = slice(part * LANES, (part + 1) * LANES)
             out_ref[slope, :, lanes] = turned_ref[slope, pl.ds(part, CB_DEV, stride=parts), :].astype(BF16)
-    for copy in copies[2:]:
+    for copy in copies:
         copy.wait()
 
 
-def image_stage(place_ref, start_ref, beams_ref, early_ref, late_ref, out_ref, *, scale, copies):
+def image_stage(
+    place_ref, start_ref, beams_ref, early_ref, middle_ref, operator_hbm, out_ref, late_ref, sems, *, scale, copies
+):
+    held = [early_ref, middle_ref, late_ref]
+    widths = [ref.shape[1] // DEPTH for ref in held]
+    arriving = started(column_copies(operator_hbm, late_ref, (widths[0] + widths[1]) * DEPTH), sems)
     live = start_ref.shape[1]
     padded = place_ref.shape[1]
-    half = early_ref.shape[1] // DEPTH
     centres = out_ref.shape[0] * out_ref.shape[2]
     pick = (lax.broadcasted_iota(jnp.int32, (live, padded), 0) == place_ref[...]).astype(F32).astype(BF16)
     chosen = jnp.dot(pick, beams_ref[...], preferred_element_type=F32).astype(BF16)
     point = lax.broadcasted_iota(jnp.int32, (centres, live), 0) - start_ref[...]
     image = jnp.zeros((centres, DEPTH), F32)
-    for step in range(2 * half):
-        columns = slice(step % half * DEPTH, (step % half + 1) * DEPTH)
-        operator_ref = early_ref if step < half else late_ref
+    steps = [(ref, column) for ref, width in zip(held, widths) for column in range(width)]
+    for step, (operator_ref, column) in enumerate(steps):
+        if step == widths[0] + widths[1]:
+            for copy in arriving:
+                copy.wait()
+        columns = slice(column * DEPTH, (column + 1) * DEPTH)
         footprint = jnp.dot(chosen, operator_ref[:, columns], preferred_element_type=F32)
         high, low = split_bf16(footprint)
         hit = (point == step).astype(F32).astype(BF16)
@@ -230,6 +237,7 @@
 
 
 VMEM = pl.BlockSpec(memory_space=pltpu.VMEM)
+SMEM = pl.BlockSpec(memory_space=pltpu.SMEM)
 HBM = pl.BlockSpec(memory_space=pltpu.HBM)
 
 
@@ -292,6 +300,8 @@
     tiles = jnp.arange(mid_count, dtype=jnp.int32)
     rows = mid_count * CB_DEV
     live_total = rows // 2
+    steps = operator.shape[1] // DEPTH
+    early_width, middle_width = (steps * share // 8 * DEPTH for share in SHARES)
     if sub_count == 1:
         odd_tile = mid_index % 2 == 1
         head, tail = own[:HALF], own[own.shape[0] - HALF :]
@@ -303,46 +313,43 @@
         parts = samples // LANES
         inner = own.shape[0] * parts
         edge = 2 * HALF * parts
-        half_shape = (operator.shape[0], operator.shape[1] // 2)
-        spec, high, low, cosine, sine, operator_early, place, live_starts = pl.pallas_call(
+        spec, high, low, cosine, sine, early, place, live_starts, count_held, centre_held = pl.pallas_call(
             first_stage,
             out_shape=[pltpu.VMEM((inner, LANES), F32)]
             + [pltpu.VMEM(t.shape, t.dtype) for t in tables]
-            + [pltpu.VMEM(half_shape, BF16)]
-            + [pltpu.VMEM((1, n), jnp.int32) for n in (rows, live_total)],
-            in_specs=[HBM] * 8,
-            out_specs=[VMEM] * 8,
+            + [pltpu.VMEM((samples, early_width), BF16)]
+            + [pltpu.VMEM((1, n), jnp.int32) for n in (rows, live_total)]
+            + [pltpu.SMEM(t.shape, jnp.int32) for t in (counts, centre_offset)],
+            in_specs=[HBM] * 9,
+            out_specs=[VMEM] * 8 + [SMEM] * 2,
             scratch_shapes=[
                 pltpu.VMEM(own.shape, BF16),
-                pltpu.SMEM(counts.shape, jnp.int32),
                 pltpu.VMEM((P_SIZE, rows), jnp.int32),
-                pltpu.SemaphoreType.DMA((7 + PIECES,)),
+                pltpu.SemaphoreType.DMA((8 + PIECES,)),
             ],
             compiler_params=limit(16),
             cost_estimate=cost(4 * 10**9, 10**7),
             name="first",
-        )(*(in_hbm(t) for t in (own,) + tables[:2] + (counts, foot_start.T) + tables[2:] + (operator,)))
-        beams, operator_late = pl.pallas_call(
-            beams_stage,
-            out_shape=[pltpu.VMEM((P_SIZE, CB_DEV, samples), BF16), pltpu.VMEM(half_shape, BF16)],
-            in_specs=[HBM] * 3 + [VMEM] * 7,
+        )(*(in_hbm(t) for t in (own,) + tables[:2] + (counts, foot_start.T, centre_offset) + tables[2:] + (operator,)))
+        beams, middle = pl.pallas_call(
+            functools.partial(beams_stage, first_column=early_width),
+            out_shape=[pltpu.VMEM((P_SIZE, CB_DEV, samples), BF16), pltpu.VMEM((samples, middle_width), BF16)],
+            in_specs=[SMEM, SMEM, HBM] + [VMEM] * 7,
             out_specs=[VMEM] * 2,
             scratch_shapes=[
                 pltpu.VMEM((edge, LANES), F32),
                 pltpu.VMEM((edge + inner, LANES), F32),
                 pltpu.VMEM((P_SIZE, CB_DEV * parts, LANES), F32),
-                pltpu.SMEM(centre_offset.shape, jnp.int32),
-                pltpu.SMEM(beam_count.shape, jnp.int32),
-                pltpu.SemaphoreType.DMA((2 + PIECES,)),
+                pltpu.SemaphoreType.DMA((PIECES,)),
             ],
             compiler_params=limit(16),
             cost_estimate=cost(4 * 10**9, 4 * 10**6),
             name="beams",
-        )(in_hbm(centre_offset), in_hbm(counts), in_hbm(operator), spec, within, across, high, low, cosine, sine)
+        )(centre_held, count_held, in_hbm(operator), spec, within, across, high, low, cosine, sine)
     else:
         live_here = jnp.sum(jnp.where(tiles == mid_index, counts, 0))
         beams = beams_split_time(own, centre_offset, live_here)
-        operator_early, operator_late = jnp.split(operator, 2, axis=1)
+        early, middle = operator[:, :early_width], operator[:, early_width : early_width + middle_width]
         first_column = mid_index * operator.shape[1]
         before = jnp.sum(jnp.where(tiles[None, :] < tiles[:, None], counts[None, :], 0), axis=1)
         slot = jnp.arange(CB_DEV, dtype=jnp.int32)
@@ -361,12 +368,16 @@
     partial_image = pl.pallas_call(
         functools.partial(image_stage, scale=1.0 / math.sqrt(FL * P_SIZE), copies=off_count),
         out_shape=jax.ShapeDtypeStruct((mid_count, off_count, CB_DEV, DEPTH), BF16),
-        in_specs=[VMEM] * 5,
+        in_specs=[VMEM] * 5 + [HBM],
         out_specs=VMEM,
+        scratch_shapes=[
+            pltpu.VMEM((samples, operator.shape[1] - early_width - middle_width), BF16),
+            pltpu.SemaphoreType.DMA((PIECES,)),
+        ],
         compiler_params=limit(24),
         cost_estimate=cost(2 * 10**9, 10**7),
         name="image",
-    )(place, live_starts, received, operator_early, operator_late)
+    )(place, live_starts, received, early, middle, in_hbm(operator))
     parts = lax.all_to_all(
         partial_image.reshape(mid_count * off_count * CB_DEV, DEPTH),
         ("mid", "off"),

time: 48.4 us -> 48.1 us (level)
  Pallas kernels: 7.96 us -> 7.37 us
where the time goes in v3:
time: 48.1 us; the launch traced here: 47.8 us
  blocking collectives  33.9 us (70%)
  Pallas kernels  7.37 us (15%)
  starting transfers between devices  5.08 us (11%)
  other arithmetic  1.43 us (3%)
    all_to_all x1, blocking collectives, shards(): lax.all_to_all(beams.reshape(mid_count * CB_DEV, samples), 'mid', split_a...  19.4 us
    all_to_all x1, blocking collectives, shards(): lax.all_to_all(partial_image.reshape(mid_count * off_count * CB_DEV, DEPT...  14.5 us
    ppermute x1, starting transfers between devices, shards(): lax.ppermute(jnp.where(odd_tile, head, tail), 'mid', [(i, i ^ 1) for i in...  4.42 us
    pallas_call x1, Pallas kernels, shards(): pl.pallas_call(functools.partial(image_stage, scale=1.0 / math.sqrt(FL *...  2.73 us
    pallas_call x1, Pallas kernels, shards(): pl.pallas_call(first_stage, out_shape=[pltpu.VMEM((inner, LANES), F32)] +...  2.69 us
    pallas_call x1, Pallas kernels, shards(): pl.pallas_call(functools.partial(beams_stage, first_column=early_width),...  1.96 us
  transfers between devices with their start and end apart: 2, of which 0 were waited for; matrix products, arithmetic and copies ran while one was open for 0% of the time, Pallas kernels for 6%

profile of v3, /device:TPU:0, one launch (start us, length us, event | category | flops | bytes accessed | tf_op | source)
XLA Modules:
  0.0 47.8 jit_solution(2078310382983384702)
XLA Ops:
  0.0 0.8 %select_bitcast_fusion = (bf16[16,1024]{1,0:T(8,128)(2,1)S(1)}, bf16[16,1024]{1,0:T(8,128)(2,1)S(1)}) fusion(pred[]{:T(512)S(6)} %eq.5, bf16[1,64,1024]{2,1,0:T(8,128)(2,1)} %param.9), kind=kLoop, calls=%fused_computation.1 | loop fusion | flops 32768 | bytes 131073 | tf_op jit(solution)/shard_map/jit(_where)/select_n | solution.py:311
  0.8 0.7 %collective-permute-start.1 = (bf16[16,1024]{1,0:T(8,128)(2,1)S(1)}, bf16[16,1024]{1,0:T(8,128)(2,1)S(1)}, u32[]{:S(2)}, u32[]{:S(2)}) collective-permute-start(bf16[16,1024]{1,0:T(8,128)(2,1)S(1)} %get-tuple-element.29), channel_id=1, source_target_pairs={{0,0},{30,30},{2,4},{4,2},{6,8},{8,6},{10,12},{12,10},{14,16},{16,... | collective-permute-start | bytes 98312 | tf_op jit(solution)/shard_map/ppermute | solution.py:311
  1.4 4.4 %collective-permute-start = (bf16[16,1024]{1,0:T(8,128)(2,1)S(1)}, bf16[16,1024]{1,0:T(8,128)(2,1)S(1)}, u32[]{:S(2)}, u32[]{:S(2)}) collective-permute-start(bf16[16,1024]{1,0:T(8,128)(2,1)S(1)} %get-tuple-element.30), channel_id=1, source_target_pairs={{0,2},{2,0},{4,6},{6,4},{8,10},{10,8},{12,14},{14,12},{16,18},{18,... | collective-permute-start | bytes 98312 | tf_op jit(solution)/shard_map/ppermute | solution.py:310
  5.9 2.7 %first.1 = (f32[512,128]{1,0:T(8,128)S(1)}, bf16[256,1024]{1,0:T(8,128)(2,1)S(1)}, bf16[256,1024]{1,0:T(8,128)(2,1)S(1)}, f32[17,8,8,128]{3,2,1,0:T(8,128)S(1)},...) custom-call(bf16[64,1024]{1,0:T(8,128)(2,1)} %bitcast.10, ...), custom_call_target="tpu_custom_call" | custom-call | flops 4000000000 | bytes 10000000 | tf_op jit(solution)/shard_map/first/pallas_call | solution.py:316
  8.6 0.0 collective-permute-done.1.across_ref
  8.6 0.0 collective-permute-done.within_ref
  8.6 2.0 %beams.1 = (bf16[16,16,1024]{2,1,0:T(8,128)(2,1)S(1)}, bf16[1024,1536]{1,0:T(8,128)(2,1)S(1)}) custom-call(s32[16]{0:T(128)S(4)} %get-tuple-element.19.centre_ref, s32[16]{0:T(128)S(4)} %get-tuple-element.20.count_ref, bf16[1024,4096]{1,0:T(8,128)(2,1)} %operator_hbm.5, f32[512,128]{1,0:T(8,128)S(1)} %get-tuple-element.21.own_spec_ref, ...), custom_call_target="tpu_custom_call" | custom-call | flops 4000000000 | bytes 4000000 | tf_op jit(solution)/shard_map/beams/pallas_call | solution.py:334
  10.5 19.4 %all_to_all.17 = bf16[16,16,1024]{2,1,0:T(8,128)(2,1)S(1)} all-to-all(bf16[16,16,1024]{2,1,0:T(8,128)(2,1)S(1)} %get-tuple-element.26), channel_id=1, replica_groups=mesh['grp'=1,'mid'=16,'off'=2,'sub'=1] {'mid'}, dimensions={0} | all-to-all | bytes 1048576 | tf_op jit(solution)/shard_map/all_to_all | solution.py:365
  29.9 2.7 %image.1 = bf16[16,2,16,256]{3,2,1,0:T(8,128)(2,1)S(1)} custom-call(s32[1,256]{1,0:T(1,128)S(1)} %get-tuple-element.17.place_ref, s32[1,128]{1,0:T(1,128)S(1)} %get-tuple-element.18.start_ref, bf16[256,1024]{1,0:T(8,128)(2,1)S(1)} %bitcast.8, bf16[1024,1536]{1,0:T(8,128)(2,1)S(1)} %get-tuple-element.27.early_ref, ...), custom_call_target="tpu_custom_call" | custom-call | flops 2000000000 | bytes 10000000 | tf_op jit(solution)/shard_map/image/pallas_call | solution.py:368
  32.6 14.5 %all_to_all.18 = bf16[32,16,256]{2,1,0:T(8,128)(2,1)S(1)} all-to-all(bf16[32,16,256]{2,1,0:T(8,128)(2,1)S(1)} %bitcast.9), channel_id=1, replica_groups=mesh['grp'=1,'mid'=16,'off'=2,'sub'=1] {'mid','off'}, dimensions={0} | all-to-all | bytes 524288 | tf_op jit(solution)/shard_map/all_to_all | solution.py:381
  47.2 0.7 %convert_reduce_fusion = f32[16,256]{1,0:T(8,128)} fusion(bf16[32,16,256]{2,1,0:T(8,128)(2,1)S(1)} %all_to_all.18), kind=kLoop, calls=%fused_computation | loop fusion | flops 258048 | bytes 278528 | tf_op jit(solution)/shard_map/reduce_sum | solution.py:388
Async XLA Ops:
  0.8 7.8 %collective-permute-start.1 = (bf16[16,1024]{1,0:T(8,128)(2,1)S(1)}, bf16[16,1024]{1,0:T(8,128)(2,1)S(1)}, u32[]{:S(2)}, u32[]{:S(2)}) collective-permute-start(bf16[16,1024]{1,0:T(8,128)(2,1)S(1)} %get-tuple-element.29), channel_id=1, source_target_pairs={{0,0},{30,30},{2,4},{4,2},{6,8},{8,6},{10,12},{12,10},{14,16},{16,... | collective-permute-start | bytes 98312 | tf_op jit(solution)/shard_map/ppermute | solution.py:311
  1.4 7.1 %collective-permute-start = (bf16[16,1024]{1,0:T(8,128)(2,1)S(1)}, bf16[16,1024]{1,0:T(8,128)(2,1)S(1)}, u32[]{:S(2)}, u32[]{:S(2)}) collective-permute-start(bf16[16,1024]{1,0:T(8,128)(2,1)S(1)} %get-tuple-element.30), channel_id=1, source_target_pairs={{0,2},{2,0},{4,6},{6,4},{8,10},{10,8},{12,14},{14,12},{16,18},{18,... | collective-permute-start | bytes 98312 | tf_op jit(solution)/shard_map/ppermute | solution.py:310

commit v4 on v3

--- a/solution.py
+++ b/solution.py
@@ -19,6 +19,7 @@
 LANES = 128
 PIECES = 4
 SHARES = (3, 3)
+BLOCKS = (2, 0, 3, 1)
 BF16 = jnp.bfloat16
 F32 = jnp.float32
 
@@ -86,17 +87,26 @@
         )
 
 
+def travel_order(count):
+    block = count // len(BLOCKS)
+    return [first * block + step for step in range(block) for first in BLOCKS]
+
+
 def live_layout(counts, starts, live):
     padded = starts.shape[1]
+    tiles = padded // CB_DEV
+    order = travel_order(tiles)
     beam = lax.broadcasted_iota(jnp.int32, (1, padded), 1)
     place = jnp.full((1, padded), -1, jnp.int32)
+    own_place = place
     before = jnp.int32(0)
-    for tile in range(padded // CB_DEV):
-        slot = beam - tile * CB_DEV
-        here = (slot >= 0) & (slot < counts[tile])
-        place = jnp.where(here, before + slot, place)
+    for tile in range(tiles):
+        own_slot = beam - tile * CB_DEV
+        slot = beam - order.index(tile) * CB_DEV
+        own_place = jnp.where((own_slot >= 0) & (own_slot < counts[tile]), before + own_slot, own_place)
+        place = jnp.where((slot >= 0) & (slot < counts[tile]), before + slot, place)
         before = before + counts[tile]
-    pick = (lax.broadcasted_iota(jnp.int32, (live, padded), 0) == place).astype(F32).astype(BF16)
+    pick = (lax.broadcasted_iota(jnp.int32, (live, padded), 0) == own_place).astype(F32).astype(BF16)
     row = lax.broadcasted_iota(jnp.int32, (8, padded), 0)
     digits = jnp.where(row == 0, starts % CB_DEV, jnp.where(row == 1, starts // CB_DEV, 0))
     digits = lax.dot_general(
@@ -194,10 +204,12 @@
         return carry
 
     lax.fori_loop(0, CB_DEV, one_beam, 0)
-    for slope in range(P_SIZE):
+    destinations = out_ref.shape[0]
+    for position, tile_index in enumerate(travel_order(destinations)):
+        slope = tile_index // (destinations // P_SIZE)
         for part in range(parts):
             lanes = slice(part * LANES, (part + 1) * LANES)
-            out_ref[slope, :, lanes] = turned_ref[slope, pl.ds(part, CB_DEV, stride=parts), :].astype(BF16)
+            out_ref[position, :, lanes] = turned_ref[slope, pl.ds(part, CB_DEV, stride=parts), :].astype(BF16)
     for copy in copies:
         copy.wait()
 
@@ -333,7 +345,7 @@
         )(*(in_hbm(t) for t in (own,) + tables[:2] + (counts, foot_start.T, centre_offset) + tables[2:] + (operator,)))
         beams, middle = pl.pallas_call(
             functools.partial(beams_stage, first_column=early_width),
-            out_shape=[pltpu.VMEM((P_SIZE, CB_DEV, samples), BF16), pltpu.VMEM((samples, middle_width), BF16)],
+            out_shape=[pltpu.VMEM((mid_count, CB_DEV, samples), BF16), pltpu.VMEM((samples, middle_width), BF16)],
             in_specs=[SMEM, SMEM, HBM] + [VMEM] * 7,
             out_specs=[VMEM] * 2,
             scratch_shapes=[
@@ -348,7 +360,8 @@
         )(centre_held, count_held, in_hbm(operator), spec, within, across, high, low, cosine, sine)
     else:
         live_here = jnp.sum(jnp.where(tiles == mid_index, counts, 0))
-        beams = beams_split_time(own, centre_offset, live_here)
+        order = np.array(travel_order(mid_count))
+        beams = beams_split_time(own, centre_offset, live_here)[order // (mid_count // P_SIZE)]
         early, middle = operator[:, :early_width], operator[:, early_width : early_width + middle_width]
         first_column = mid_index * operator.shape[1]
         before = jnp.sum(jnp.where(tiles[None, :] < tiles[:, None], counts[None, :], 0), axis=1)
@@ -359,11 +372,14 @@
         here = place.reshape(rows, 1) == position[None, :]
         live_starts = jnp.sum(jnp.where(here, starts[:, None], 0), axis=0)
         live_starts = (live_starts + first_column % (FL * DEPTH) // DEPTH).reshape(1, live_total)
-    shares = mid_count // P_SIZE
-    if shares > 1:
-        beams = jnp.repeat(beams, shares, axis=0)
+        place = place.reshape(mid_count, CB_DEV)[order].reshape(1, rows)
     received = lax.all_to_all(
-        beams.reshape(mid_count * CB_DEV, samples), "mid", split_axis=0, concat_axis=0, tiled=True
+        beams.reshape(rows, samples),
+        "mid",
+        split_axis=0,
+        concat_axis=0,
+        tiled=True,
+        axis_index_groups=[travel_order(mid_count)],
     )
     partial_image = pl.pallas_call(
         functools.partial(image_stage, scale=1.0 / math.sqrt(FL * P_SIZE), copies=off_count),

time: 48.1 us -> 47.7 us (level)
    all_to_all x1, blocking collectives: 19.4 us -> 17.9 us  [shards(): lax.all_to_all(beams.reshape(rows, samples), 'mid', split_axis=0, concat_...]
    all_to_all x1, blocking collectives: 14.5 us -> 15.7 us  [shards(): lax.all_to_all(partial_image.reshape(mid_count * off_count * CB_DEV, DEPT...]
where the time goes in v4:
time: 47.7 us; the launch traced here: 47.5 us
  blocking collectives  33.6 us (70%)
  Pallas kernels  7.37 us (15%)
  starting transfers between devices  5.08 us (11%)
  other arithmetic  1.43 us (3%)
    all_to_all x1, blocking collectives, shards(): lax.all_to_all(beams.reshape(rows, samples), 'mid', split_axis=0, concat_...  17.9 us
    all_to_all x1, blocking collectives, shards(): lax.all_to_all(partial_image.reshape(mid_count * off_count * CB_DEV, DEPT...  15.7 us
    ppermute x1, starting transfers between devices, shards(): lax.ppermute(jnp.where(odd_tile, head, tail), 'mid', [(i, i ^ 1) for i in...  4.42 us
    pallas_call x1, Pallas kernels, shards(): pl.pallas_call(functools.partial(image_stage, scale=1.0 / math.sqrt(FL *...  2.73 us
    pallas_call x1, Pallas kernels, shards(): pl.pallas_call(first_stage, out_shape=[pltpu.VMEM((inner, LANES), F32)] +...  2.69 us
    pallas_call x1, Pallas kernels, shards(): pl.pallas_call(functools.partial(beams_stage, first_column=early_width),...  1.96 us
  transfers between devices with their start and end apart: 2, of which 0 were waited for; matrix products, arithmetic and copies ran while one was open for 0% of the time, Pallas kernels for 6%

profile of v4, /device:TPU:0, one launch (start us, length us, event | category | flops | bytes accessed | tf_op | source)
XLA Modules:
  0.0 47.5 jit_solution(15175925087340251736)
XLA Ops:
  0.0 0.8 %select_bitcast_fusion = (bf16[16,1024]{1,0:T(8,128)(2,1)S(1)}, bf16[16,1024]{1,0:T(8,128)(2,1)S(1)}) fusion(pred[]{:T(512)S(6)} %eq.5, bf16[1,64,1024]{2,1,0:T(8,128)(2,1)} %param.9), kind=kLoop, calls=%fused_computation.1 | loop fusion | flops 32768 | bytes 131073 | tf_op jit(solution)/shard_map/jit(_where)/select_n | solution.py:323
  0.8 0.7 %collective-permute-start.1 = (bf16[16,1024]{1,0:T(8,128)(2,1)S(1)}, bf16[16,1024]{1,0:T(8,128)(2,1)S(1)}, u32[]{:S(2)}, u32[]{:S(2)}) collective-permute-start(bf16[16,1024]{1,0:T(8,128)(2,1)S(1)} %get-tuple-element.29), channel_id=1, source_target_pairs={{0,0},{30,30},{2,4},{4,2},{6,8},{8,6},{10,12},{12,10},{14,16},{16,... | collective-permute-start | bytes 98312 | tf_op jit(solution)/shard_map/ppermute | solution.py:323
  1.4 4.4 %collective-permute-start = (bf16[16,1024]{1,0:T(8,128)(2,1)S(1)}, bf16[16,1024]{1,0:T(8,128)(2,1)S(1)}, u32[]{:S(2)}, u32[]{:S(2)}) collective-permute-start(bf16[16,1024]{1,0:T(8,128)(2,1)S(1)} %get-tuple-element.30), channel_id=1, source_target_pairs={{0,2},{2,0},{4,6},{6,4},{8,10},{10,8},{12,14},{14,12},{16,18},{18,... | collective-permute-start | bytes 98312 | tf_op jit(solution)/shard_map/ppermute | solution.py:322
  5.9 2.7 %first.1 = (f32[512,128]{1,0:T(8,128)S(1)}, bf16[256,1024]{1,0:T(8,128)(2,1)S(1)}, bf16[256,1024]{1,0:T(8,128)(2,1)S(1)}, f32[17,8,8,128]{3,2,1,0:T(8,128)S(1)},...) custom-call(bf16[64,1024]{1,0:T(8,128)(2,1)} %bitcast.10, ...), custom_call_target="tpu_custom_call" | custom-call | flops 4000000000 | bytes 10000000 | tf_op jit(solution)/shard_map/first/pallas_call | solution.py:328
  8.6 0.0 collective-permute-done.1.across_ref
  8.6 0.0 collective-permute-done.within_ref
  8.6 2.0 %beams.1 = (bf16[16,16,1024]{2,1,0:T(8,128)(2,1)S(1)}, bf16[1024,1536]{1,0:T(8,128)(2,1)S(1)}) custom-call(s32[16]{0:T(128)S(4)} %get-tuple-element.19.centre_ref, s32[16]{0:T(128)S(4)} %get-tuple-element.20.count_ref, bf16[1024,4096]{1,0:T(8,128)(2,1)} %operator_hbm.5, f32[512,128]{1,0:T(8,128)S(1)} %get-tuple-element.21.own_spec_ref, ...), custom_call_target="tpu_custom_call" | custom-call | flops 4000000000 | bytes 4000000 | tf_op jit(solution)/shard_map/beams/pallas_call | solution.py:346
  10.5 17.9 %all_to_all.17 = bf16[16,16,1024]{2,1,0:T(8,128)(2,1)S(1)} all-to-all(bf16[16,16,1024]{2,1,0:T(8,128)(2,1)S(1)} %get-tuple-element.26), channel_id=1, replica_groups={{16,0,24,8,18,2,26,10,20,4,28,12,22,6,30,14},{17,1,25,9,19,3,27,11,21,5..., dimensions={0} | all-to-all | bytes 1048576 | tf_op jit(solution)/shard_map/all_to_all | solution.py:376
  28.5 2.7 %image.1 = bf16[16,2,16,256]{3,2,1,0:T(8,128)(2,1)S(1)} custom-call(s32[1,256]{1,0:T(1,128)S(1)} %get-tuple-element.17.place_ref, s32[1,128]{1,0:T(1,128)S(1)} %get-tuple-element.18.start_ref, bf16[256,1024]{1,0:T(8,128)(2,1)S(1)} %bitcast.8, bf16[1024,1536]{1,0:T(8,128)(2,1)S(1)} %get-tuple-element.27.early_ref, ...), custom_call_target="tpu_custom_call" | custom-call | flops 2000000000 | bytes 10000000 | tf_op jit(solution)/shard_map/image/pallas_call | solution.py:384
  31.2 15.7 %all_to_all.18 = bf16[32,16,256]{2,1,0:T(8,128)(2,1)S(1)} all-to-all(bf16[32,16,256]{2,1,0:T(8,128)(2,1)S(1)} %bitcast.9), channel_id=1, replica_groups=mesh['grp'=1,'mid'=16,'off'=2,'sub'=1] {'mid','off'}, dimensions={0} | all-to-all | bytes 524288 | tf_op jit(solution)/shard_map/all_to_all | solution.py:397
  46.9 0.7 %convert_reduce_fusion = f32[16,256]{1,0:T(8,128)} fusion(bf16[32,16,256]{2,1,0:T(8,128)(2,1)S(1)} %all_to_all.18), kind=kLoop, calls=%fused_computation | loop fusion | flops 258048 | bytes 278528 | tf_op jit(solution)/shard_map/reduce_sum | solution.py:404
Async XLA Ops:
  0.8 7.8 %collective-permute-start.1 = (bf16[16,1024]{1,0:T(8,128)(2,1)S(1)}, bf16[16,1024]{1,0:T(8,128)(2,1)S(1)}, u32[]{:S(2)}, u32[]{:S(2)}) collective-permute-start(bf16[16,1024]{1,0:T(8,128)(2,1)S(1)} %get-tuple-element.29), channel_id=1, source_target_pairs={{0,0},{30,30},{2,4},{4,2},{6,8},{8,6},{10,12},{12,10},{14,16},{16,... | collective-permute-start | bytes 98312 | tf_op jit(solution)/shard_map/ppermute | solution.py:323
  1.4 7.1 %collective-permute-start = (bf16[16,1024]{1,0:T(8,128)(2,1)S(1)}, bf16[16,1024]{1,0:T(8,128)(2,1)S(1)}, u32[]{:S(2)}, u32[]{:S(2)}) collective-permute-start(bf16[16,1024]{1,0:T(8,128)(2,1)S(1)} %get-tuple-element.30), channel_id=1, source_target_pairs={{0,2},{2,0},{4,6},{6,4},{8,10},{10,8},{12,14},{14,12},{16,18},{18,... | collective-permute-start | bytes 98312 | tf_op jit(solution)/shard_map/ppermute | solution.py:322

commit v5 on v4

--- a/solution.py
+++ b/solution.py
@@ -19,7 +19,7 @@
 LANES = 128
 PIECES = 4
 SHARES = (3, 3)
-BLOCKS = (2, 0, 3, 1)
+BLOCKS = (1, 3, 0, 2)
 BF16 = jnp.bfloat16
 F32 = jnp.float32
 

time: 47.7 us -> 46.8 us (0.981)
  blocking collectives: 33.6 us -> 32.2 us
    all_to_all x1, blocking collectives: 15.7 us -> 13.2 us  [shards(): lax.all_to_all(partial_image.reshape(mid_count * off_count * CB_DEV, DEPT...]
    all_to_all x1, blocking collectives: 17.9 us -> 19 us  [shards(): lax.all_to_all(beams.reshape(rows, samples), 'mid', split_axis=0, concat_...]
where the time goes in v5:
time: 46.8 us; the launch traced here: 46.5 us
  blocking collectives  32.2 us (69%)
  Pallas kernels  7.73 us (17%)
  starting transfers between devices  5.08 us (11%)
  other arithmetic  1.43 us (3%)
    all_to_all x1, blocking collectives, shards(): lax.all_to_all(beams.reshape(rows, samples), 'mid', split_axis=0, concat_...  19 us
    all_to_all x1, blocking collectives, shards(): lax.all_to_all(partial_image.reshape(mid_count * off_count * CB_DEV, DEPT...  13.2 us
    ppermute x1, starting transfers between devices, shards(): lax.ppermute(jnp.where(odd_tile, head, tail), 'mid', [(i, i ^ 1) for i in...  4.42 us
    pallas_call x1, Pallas kernels, shards(): pl.pallas_call(functools.partial(image_stage, scale=1.0 / math.sqrt(FL *...  2.73 us
    pallas_call x1, Pallas kernels, shards(): pl.pallas_call(first_stage, out_shape=[pltpu.VMEM((inner, LANES), F32)] +...  2.69 us
    pallas_call x1, Pallas kernels, shards(): pl.pallas_call(functools.partial(beams_stage, first_column=early_width),...  2.32 us
  transfers between devices with their start and end apart: 2, of which 0 were waited for; matrix products, arithmetic and copies ran while one was open for 0% of the time, Pallas kernels for 6%

profile of v5, /device:TPU:0, one launch (start us, length us, event | category | flops | bytes accessed | tf_op | source)
XLA Modules:
  0.0 46.5 jit_solution(8472314387237467582)
XLA Ops:
  0.0 0.8 %select_bitcast_fusion = (bf16[16,1024]{1,0:T(8,128)(2,1)S(1)}, bf16[16,1024]{1,0:T(8,128)(2,1)S(1)}) fusion(pred[]{:T(512)S(6)} %eq.5, bf16[1,64,1024]{2,1,0:T(8,128)(2,1)} %param.9), kind=kLoop, calls=%fused_computation.1 | loop fusion | flops 32768 | bytes 131073 | tf_op jit(solution)/shard_map/jit(_where)/select_n | solution.py:323
  0.8 0.7 %collective-permute-start.1 = (bf16[16,1024]{1,0:T(8,128)(2,1)S(1)}, bf16[16,1024]{1,0:T(8,128)(2,1)S(1)}, u32[]{:S(2)}, u32[]{:S(2)}) collective-permute-start(bf16[16,1024]{1,0:T(8,128)(2,1)S(1)} %get-tuple-element.29), channel_id=1, source_target_pairs={{0,0},{30,30},{2,4},{4,2},{6,8},{8,6},{10,12},{12,10},{14,16},{16,... | collective-permute-start | bytes 98312 | tf_op jit(solution)/shard_map/ppermute | solution.py:323
  1.4 4.4 %collective-permute-start = (bf16[16,1024]{1,0:T(8,128)(2,1)S(1)}, bf16[16,1024]{1,0:T(8,128)(2,1)S(1)}, u32[]{:S(2)}, u32[]{:S(2)}) collective-permute-start(bf16[16,1024]{1,0:T(8,128)(2,1)S(1)} %get-tuple-element.30), channel_id=1, source_target_pairs={{0,2},{2,0},{4,6},{6,4},{8,10},{10,8},{12,14},{14,12},{16,18},{18,... | collective-permute-start | bytes 98312 | tf_op jit(solution)/shard_map/ppermute | solution.py:322
  5.9 2.7 %first.1 = (f32[512,128]{1,0:T(8,128)S(1)}, bf16[256,1024]{1,0:T(8,128)(2,1)S(1)}, bf16[256,1024]{1,0:T(8,128)(2,1)S(1)}, f32[17,8,8,128]{3,2,1,0:T(8,128)S(1)},...) custom-call(bf16[64,1024]{1,0:T(8,128)(2,1)} %bitcast.10, ...), custom_call_target="tpu_custom_call" | custom-call | flops 4000000000 | bytes 10000000 | tf_op jit(solution)/shard_map/first/pallas_call | solution.py:328
  8.6 0.0 collective-permute-done.1.across_ref
  8.6 0.0 collective-permute-done.within_ref
  8.6 2.3 %beams.1 = (bf16[16,16,1024]{2,1,0:T(8,128)(2,1)S(1)}, bf16[1024,1536]{1,0:T(8,128)(2,1)S(1)}) custom-call(s32[16]{0:T(128)S(4)} %get-tuple-element.19.centre_ref, s32[16]{0:T(128)S(4)} %get-tuple-element.20.count_ref, bf16[1024,4096]{1,0:T(8,128)(2,1)} %operator_hbm.5, f32[512,128]{1,0:T(8,128)S(1)} %get-tuple-element.21.own_spec_ref, ...), custom_call_target="tpu_custom_call" | custom-call | flops 4000000000 | bytes 4000000 | tf_op jit(solution)/shard_map/beams/pallas_call | solution.py:346
  10.9 19.0 %all_to_all.17 = bf16[16,16,1024]{2,1,0:T(8,128)(2,1)S(1)} all-to-all(bf16[16,16,1024]{2,1,0:T(8,128)(2,1)S(1)} %get-tuple-element.26), channel_id=1, replica_groups={{8,24,0,16,10,26,2,18,12,28,4,20,14,30,6,22},{9,25,1,17,11,27,3,19,13,2..., dimensions={0} | all-to-all | bytes 1048576 | tf_op jit(solution)/shard_map/all_to_all | solution.py:376
  29.9 2.7 %image.1 = bf16[16,2,16,256]{3,2,1,0:T(8,128)(2,1)S(1)} custom-call(s32[1,256]{1,0:T(1,128)S(1)} %get-tuple-element.17.place_ref, s32[1,128]{1,0:T(1,128)S(1)} %get-tuple-element.18.start_ref, bf16[256,1024]{1,0:T(8,128)(2,1)S(1)} %bitcast.8, bf16[1024,1536]{1,0:T(8,128)(2,1)S(1)} %get-tuple-element.27.early_ref, ...), custom_call_target="tpu_custom_call" | custom-call | flops 2000000000 | bytes 10000000 | tf_op jit(solution)/shard_map/image/pallas_call | solution.py:384
  32.6 13.2 %all_to_all.18 = bf16[32,16,256]{2,1,0:T(8,128)(2,1)S(1)} all-to-all(bf16[32,16,256]{2,1,0:T(8,128)(2,1)S(1)} %bitcast.9), channel_id=1, replica_groups=mesh['grp'=1,'mid'=16,'off'=2,'sub'=1] {'mid','off'}, dimensions={0} | all-to-all | bytes 524288 | tf_op jit(solution)/shard_map/all_to_all | solution.py:397
  45.9 0.7 %convert_reduce_fusion = f32[16,256]{1,0:T(8,128)} fusion(bf16[32,16,256]{2,1,0:T(8,128)(2,1)S(1)} %all_to_all.18), kind=kLoop, calls=%fused_computation | loop fusion | flops 258048 | bytes 278528 | tf_op jit(solution)/shard_map/reduce_sum | solution.py:404
Async XLA Ops:
  0.8 7.8 %collective-permute-start.1 = (bf16[16,1024]{1,0:T(8,128)(2,1)S(1)}, bf16[16,1024]{1,0:T(8,128)(2,1)S(1)}, u32[]{:S(2)}, u32[]{:S(2)}) collective-permute-start(bf16[16,1024]{1,0:T(8,128)(2,1)S(1)} %get-tuple-element.29), channel_id=1, source_target_pairs={{0,0},{30,30},{2,4},{4,2},{6,8},{8,6},{10,12},{12,10},{14,16},{16,... | collective-permute-start | bytes 98312 | tf_op jit(solution)/shard_map/ppermute | solution.py:323
  1.4 7.1 %collective-permute-start = (bf16[16,1024]{1,0:T(8,128)(2,1)S(1)}, bf16[16,1024]{1,0:T(8,128)(2,1)S(1)}, u32[]{:S(2)}, u32[]{:S(2)}) collective-permute-start(bf16[16,1024]{1,0:T(8,128)(2,1)S(1)} %get-tuple-element.30), channel_id=1, source_target_pairs={{0,2},{2,0},{4,6},{6,4},{8,10},{10,8},{12,14},{14,12},{16,18},{18,... | collective-permute-start | bytes 98312 | tf_op jit(solution)/shard_map/ppermute | solution.py:322
